TPU v7x, 256 devices: a whole 4x4x8 slice. The times are simulated.
256 devices in a mesh: dp: 8 (over y, core), vocab: 32 (over x, z).
Axes of the slice: x: 4, y: 4, z: 8, core: 2. Of those that a mesh axis runs over, the one named last changes fastest.
Arguments:
- hidden: bfloat16 [512, 3584], P('dp'), may hold values from -48 to 48
- embedding: bfloat16 [196608, 3584], P(('dp', 'vocab')), may hold values from -1 to 1
- targets: int32 [512], P('dp'), may hold values from 0 to 196607
- loss_weight: bfloat16 [512], P('dp'), may hold values from 1 to 10
Outputs:
- hidden_grad: bfloat16 [512, 3584], P('dp')
- table_grad: bfloat16 [196608, 3584], P(('dp', 'vocab'))
All inputs are finite; a program needn't handle non-finite values.
Results may differ from a plain program's by a relative error of at most 0.0049.
Values may be sent and summed in bfloat16 or wider, within the bound.
A program may use at most 128 MiB of HBM per device.

v0:
```python
import jax
import jax.numpy as jnp
from jax import lax
from jax.sharding import Mesh
from jax.sharding import PartitionSpec as P

DP = ("dp_0", "dp_1")
VOCAB = ("vocab_0", "vocab_1")
DP_VOCAB = ("dp_0", "dp_1", "vocab_0", "vocab_1")


soft_cap = 30.0
z_weight = 0.002


def in_one_piece(arrays, axis, dim, along):
    columns = [a.reshape(*a.shape[:along], -1) for a in arrays]
    both = jnp.concatenate(columns, axis=along)
    result, at, outs = (lax.all_gather(both, axis, axis=dim, tiled=True), 0, [])
    for a, column in zip(arrays, columns):
        slab = result[..., at : at + column.shape[along]]
        outs.append(slab.reshape(*slab.shape[:along], *a.shape[along:]))
        at += column.shape[along]
    return tuple(outs)


def from_everyone(x, axis):
    copies = jnp.broadcast_to(x, (lax.axis_size(axis), *x.shape))
    return lax.all_to_all(copies, axis, split_axis=0, concat_axis=0, tiled=True)


def joined_along(parts, dim):
    dims = list(parts.shape[1:])
    dims[dim] *= parts.shape[0]
    return jnp.moveaxis(parts, 0, dim).reshape(dims)


def gathered_copies(x, axis, dim):
    parts = from_everyone(x, axis)
    return joined_along(parts, dim)


def over_axes(x, axes):
    for axis in axes:
        x = lax.psum(x, axis)
    return x


def body(hidden, embedding, targets, loss_weight):
    shard_rows = embedding.shape[0]
    group_hidden, group_weight = in_one_piece((hidden, loss_weight), DP, 0, 1)
    group_targets = gathered_copies(targets, DP, 0)
    logits = lax.dot_general(
        group_hidden, embedding, (((1,), (1,)), ((), ())), preferred_element_type=jnp.float32
    )
    capped = soft_cap * jnp.tanh(logits / soft_cap)
    exp_terms = jnp.exp(capped - soft_cap)
    partial_value = jnp.sum(exp_terms, axis=1)
    weight = group_weight.astype(jnp.float32)
    device_place = lax.axis_index(DP) * lax.axis_size(VOCAB) + lax.axis_index(VOCAB)
    exp_total = over_axes(partial_value, DP_VOCAB)
    factor = weight * (1.0 + 2.0 * z_weight * (soft_cap + jnp.log(exp_total))) / exp_total
    columns = device_place * shard_rows + lax.iota(jnp.int32, shard_rows)
    target_hit = group_targets[:, None] == columns[None, :]
    softmax_part = factor[:, None] * exp_terms - jnp.where(target_hit, weight[:, None], 0.0)
    scores_grad = (softmax_part * (1.0 - (capped / soft_cap) ** 2)).astype(jnp.bfloat16)
    table_grad = lax.dot_general(
        scores_grad, group_hidden, (((0,), (0,)), ((), ())), preferred_element_type=jnp.float32
    ).astype(jnp.bfloat16)
    own_rows = lax.psum_scatter(
        jnp.dot(scores_grad, embedding, preferred_element_type=jnp.float32),
        DP_VOCAB,
        scatter_dimension=0,
        tiled=True,
    )
    hidden_grad = gathered_copies(own_rows.astype(jnp.bfloat16), VOCAB, 0)
    return (hidden_grad, table_grad)


def solution(mesh):
    finer = Mesh(mesh.devices.reshape(4, 2, 4, 8), ("dp_0", "dp_1", "vocab_0", "vocab_1"))
    return jax.shard_map(
        body,
        mesh=finer,
        in_specs=(P(DP, None), P(DP_VOCAB, None), P(DP), P(DP)),
        out_specs=(P(DP, None), P(DP_VOCAB, None)),
        check_vma=False,
    )
```

profile of v0, /device:TPU:2, one launch (start us, length us, event | category | flops | bytes accessed | tf_op | source)
XLA Modules:
  0.0 269.9 jit_solution(10449393650248574156)
XLA Ops:
  7.2 0.0 all-gather.2.cloned.1.call-start
  7.2 0.8 copy.8
  8.0 1.8 pad_maximum_fusion
  9.8 0.0 all-gather.2.cloned.1.call-update
  9.8 1.3 broadcast_in_dim.22
  11.1 4.5 %all-to-all-start = ((s32[8,1,64]{2,1,0:T(1,128)}), s32[8,1,64]{2,1,0:T(1,128)S(1)}, u32[]{:S(2)}, u32[]{:S(2)}) async-start(s32[8,1,64]{2,1,0:T(1,128)} %broadcast_in_dim.22), calls=%async_computation | async-start | bytes 8192 | tf_op jit(solution)/shard_map/all_to_all | solution.py:29
  15.6 5.2 %all-to-all-done = s32[8,1,64]{2,1,0:T(1,128)S(1)} async-done(((s32[8,1,64]{2,1,0:T(1,128)}), s32[8,1,64]{2,1,0:T(1,128)S(1)}, u32[]{:S(2)}, u32[]{:S(2)}) %all-to-all-start) | async-done | bytes 2080 | tf_op jit(solution)/shard_map/all_to_all | solution.py:29
  20.8 0.5 broadcast.35
  21.3 0.7 reduce.5
  21.9 0.1 eq.15
  22.0 24.3 %all-gather.2.cloned.1.call-done = bf16[512,3585]{1,0:T(8,128)(2,1)} async-done(((bf16[64,3585]{1,0:T(8,128)(2,1)}), bf16[512,3585]{1,0:T(8,128)(2,1)}) %all-gather.2.cloned.1.call-update) | async-done | bytes 3671056 | tf_op jit(solution)/shard_map/all_gather | solution.py:19
  46.4 6.9 %fusion.3 = (f32[512]{0:T(512)S(1)}, f32[512,768]{1,0:T(8,128)S(1)}) fusion(bf16[768,3584]{1,0:T(8,128)(2,1)} %param.5, bf16[512,3585]{1,0:T(8,128)(2,1)} %all-gather.2.cloned.1.call-done), kind=kOutput, calls=%fused_computation.6 | convolution fusion | flops 2820144640 | bytes 10749952 | tf_op jit(solution)/shard_map/dot_general | solution.py:53
  53.3 8.6 %psum.28 = f32[512]{0:T(512)S(1)} all-reduce(f32[512]{0:T(512)S(1)} %get-tuple-element.2), channel_id=1, replica_groups=mesh['dp_0'=4,'dp_1'=2,'vocab_0'=4,'vocab_1'=8] {'dp_0'}, use_global_device_ids=true, to_apply=%region_1.0 | all-reduce | flops 512 | bytes 4096 | tf_op jit(solution)/shard_map/psum | solution.py:45
  61.9 2.5 psum.29
  64.4 8.6 %psum.30 = f32[512]{0:T(512)S(1)} all-reduce(f32[512]{0:T(512)S(1)} %psum.29), channel_id=1, replica_groups=mesh['dp_0'=4,'dp_1'=2,'vocab_0'=4,'vocab_1'=8] {'vocab_0'}, use_global_device_ids=true, to_apply=%region_3.0 | all-reduce | flops 512 | bytes 4096 | tf_op jit(solution)/shard_map/psum | solution.py:45
  72.9 17.4 %psum.31 = f32[512]{0:T(512)S(1)} all-reduce(f32[512]{0:T(512)S(1)} %psum.30), channel_id=1, replica_groups=mesh['dp_0'=4,'dp_1'=2,'vocab_0'=4,'vocab_1'=8] {'vocab_1'}, use_global_device_ids=true, to_apply=%region_4.0 | all-reduce | flops 512 | bytes 4096 | tf_op jit(solution)/shard_map/psum | solution.py:45
  90.4 1.0 convert_reduce_fusion
  91.4 8.1 %fusion.6 = f32[512,3584]{1,0:T(8,128)} fusion(bf16[768,3584]{1,0:T(8,128)(2,1)} %param.5, f32[512,768]{1,0:T(8,128)S(1)} %get-tuple-element.3, f32[512]{0:T(512)S(1)} %convert_reduce_fusion, s32[768]{0:T(1024)S(1)} %iota_add_fusion, f32[512]{0:T(512)S(1)} %multiply_divide_fusion, s32[512]{0:T(512)S(1)} %eq.15), kind=kOutput, calls=%fused_computation.13 | convolution fusion | flops 2822504448 | bytes 14427136 | tf_op jit(solution)/shard_map/dot_general | solution.py:71
  99.5 138.5 %all-reduce.2 = bf16[512,3584]{1,0:T(8,128)(2,1)} all-reduce(f32[512,3584]{1,0:T(8,128)} %fusion.6), channel_id=2, replica_groups=mesh['dp_0'=4,'dp_1'=2,'vocab_0'=4,'vocab_1'=8] {'dp_0','dp_1','vocab_0'..., use_global_device_ids=true, to_apply=%region_5.6.clone | all-reduce | flops 1835008 | bytes 11010048
  238.0 0.8 dynamic-slice_convert_fusion
  238.8 1.0 broadcast_in_dim.25
  239.8 7.6 %all-to-all-start.1 = ((bf16[32,2,3584]{2,1,0:T(2,128)(2,1)}), bf16[32,2,3584]{2,1,0:T(2,128)(2,1)S(1)}, u32[]{:S(2)}, u32[]{:S(2)}) async-start(bf16[32,2,3584]{2,1,0:T(2,128)(2,1)} %broadcast_in_dim.25), calls=%async_computation.1 | async-start | bytes 917504 | tf_op jit(solution)/shard_map/all_to_all | solution.py:29
  247.5 7.8 %convolution_convert_fusion = bf16[768,3584]{1,0:T(8,128)(2,1)} fusion(bf16[512,3585]{1,0:T(8,128)(2,1)} %all-gather.2.cloned.1.call-done, f32[512,768]{1,0:T(8,128)S(1)} %get-tuple-element.3, f32[512]{0:T(512)S(1)} %convert_reduce_fusion, s32[768]{0:T(1024)S(1)} %iota_add_fusion, f32[512]{0:T(512)S(1)} %multiply_divide_fusion, s32[512]{0:T(512)S(1)} %eq.15), kind=kOutput, calls=%fused_computation | convolution fusion | flops 2825256960 | bytes 10757120 | tf_op jit(solution)/shard_map/dot_general | solution.py:67
  255.2 6.9 %all-to-all-done.1 = bf16[32,2,3584]{2,1,0:T(2,128)(2,1)S(1)} async-done(((bf16[32,2,3584]{2,1,0:T(2,128)(2,1)}), bf16[32,2,3584]{2,1,0:T(2,128)(2,1)S(1)}, u32[]{:S(2)}, u32[]{:S(2)}) %all-to-all-start.1) | async-done | bytes 458784 | tf_op jit(solution)/shard_map/all_to_all | solution.py:29
  262.1 0.9 reshape.25
  (2 shorter events, 0.0 us)
Async XLA Ops:
  7.2 39.2 %all-gather.2.cloned.1.call-start = ((), (), s32[]{:S(2)}) async-start(), calls=%async_computation.2 | async-start | bytes 4276224 | tf_op jit(solution)/shard_map/all_gather | solution.py:19
  11.1 9.7 %all-to-all-start = ((s32[8,1,64]{2,1,0:T(1,128)}), s32[8,1,64]{2,1,0:T(1,128)S(1)}, u32[]{:S(2)}, u32[]{:S(2)}) async-start(s32[8,1,64]{2,1,0:T(1,128)} %broadcast_in_dim.22), calls=%async_computation | async-start | bytes 8192 | tf_op jit(solution)/shard_map/all_to_all | solution.py:29
  239.8 22.3 %all-to-all-start.1 = ((bf16[32,2,3584]{2,1,0:T(2,128)(2,1)}), bf16[32,2,3584]{2,1,0:T(2,128)(2,1)S(1)}, u32[]{:S(2)}, u32[]{:S(2)}) async-start(bf16[32,2,3584]{2,1,0:T(2,128)(2,1)} %broadcast_in_dim.25), calls=%async_computation.1 | async-start | bytes 917504 | tf_op jit(solution)/shard_map/all_to_all | solution.py:29
Sparse Core Ops, SparseCore 0:
  10.4 35.9 all-gather.1
where the time goes:
time: 272 us; the launch traced here: 270 us
  blocking collectives  176 us (65%)
  waiting for transfers between devices  36.5 us (13%)
  matrix products  22.8 us (8%)
  between operations  14.1 us (5%)
  starting transfers between devices  12.1 us (4%)
  local copies, waits for them, and re-layouts  5.38 us (2%)
  other arithmetic  3.52 us (1%)
    unnamed x1, blocking collectives  139 us
    psum x4, blocking collectives, over_axes(): x = lax.psum(x, axis)  37.1 us
    all_gather x1, waiting for transfers between devices, in_one_piece(): result, at, outs = (lax.all_gather(both, axis, axis=dim, tiled=True), 0, [])  24.3 us
    all_to_all x2, waiting for transfers between devices, from_everyone(): return lax.all_to_all(copies, axis, split_axis=0, concat_axis=0, tiled=True)  12.1 us
    all_to_all x2, starting transfers between devices, from_everyone(): return lax.all_to_all(copies, axis, split_axis=0, concat_axis=0, tiled=True)  12.1 us
    dot_general x1, matrix products, body(): jnp.dot(scores_grad, embedding, preferred_element_type=jnp.float32)  8.06 us
    dot_general x1, matrix products, body(): lax.dot_general(scores_grad, group_hidden, (((0,), (0,)), ((), ())), pref...  7.76 us
    dot_general x1, matrix products, body(): lax.dot_general(group_hidden, embedding, (((1,), (1,)), ((), ())), prefer...  6.95 us
  transfers between devices with their start and end apart: 3, of which 3 were waited for; matrix products, arithmetic and copies ran while one was open for 4% of the time, Pallas kernels for 0%

commit v1 on v0

v1 whole, which is shorter than its diff:
```python
import functools

import jax
import jax.numpy as jnp
from jax import lax
from jax.experimental import pallas as pl
from jax.experimental.pallas import tpu as pltpu
from jax.sharding import Mesh
from jax.sharding import PartitionSpec as P

MESH = pl.DeviceIdType.MESH
f32, bf16 = jnp.float32, jnp.bfloat16

NY, NC, NX, NZ = 4, 2, 4, 8
D, VROWS, ROWS = 3584, 768, 64
TOKENS = ROWS * NY * NC
HALF = ROWS * NY
BLK = D // NX
SUB = ROWS // 2
ZR = ROWS // NZ
ORDER = (2, 1, 3, 0)

soft_cap = 30.0
z_weight = 0.002


def kernel(
    hid_in, emb_in, w_in, t_in, hg_out, tg_out,
    hid, emb, wtb, wrep, trep, logit, quad, sums, stat, stat2, stat3, frep, b1, b2, b3,
    sc, sct, own, dsend, drecv, xs, ry, rx, ys, xs2, sy, sx, zs, rz, gz, gx, stage,
    local_sem, send_sem, ra, rd, rw, rb, rdd, rsy, rsx, rty, rtx, rzs, rzg, rxg, tg_sem,
):
    y, c, x, z = (lax.axis_index(a) for a in ("y", "c", "x", "z"))
    rem = lax.rem

    def at(i, n):
        return rem(i + n, n)

    sends = []

    def start(src, dst, rsem, **dev):
        copy = pltpu.make_async_remote_copy(
            src_ref=src, dst_ref=dst, send_sem=send_sem.at[len(sends)], recv_sem=rsem, device_id=dev, device_id_type=MESH
        )
        copy.start()
        sends.append(copy)

    def arrived(dst, rsem):
        pltpu.make_async_remote_copy(
            src_ref=dst, dst_ref=dst, send_sem=send_sem.at[0], recv_sem=rsem, device_id={"c": 1 - c}, device_id_type=MESH
        ).wait_recv()

    def cols(q):
        return pl.ds(pl.multiple_of(q * BLK, 128), BLK)

    def piece(cc, yy, q):
        return hid.at[pl.ds(pl.multiple_of((cc * NY + yy) * ROWS, ROWS), ROWS), cols(q)]

    def shard(cc, yy):
        return hid.at[pl.ds(pl.multiple_of((cc * NY + yy) * ROWS, ROWS), ROWS)]

    load_own = pltpu.make_async_copy(hid_in, shard(c, y), local_sem.at[0])
    load_own.start()
    load_emb = []
    for k in range(NX):
        part = pl.ds(k * (VROWS // NX), VROWS // NX)
        load_emb.append(pltpu.make_async_copy(emb_in.at[part], emb.at[part], local_sem.at[1 + k]))
        load_emb[-1].start()

    barrier = pltpu.get_barrier_semaphore()
    yc_peers = [(dy, dc) for dy in range(NY) for dc in range(NC) if (dy, dc) != (0, 0)]
    for dy, dc in yc_peers:
        pl.semaphore_signal(barrier, inc=1, device_id={"y": at(y + dy, NY), "c": at(c + dc, NC)}, device_id_type=MESH)
    for d in range(1, NX):
        pl.semaphore_signal(barrier, inc=1, device_id={"x": at(x + d, NX)}, device_id_type=MESH)
    for d in range(1, NZ):
        pl.semaphore_signal(barrier, inc=1, device_id={"z": at(z + d, NZ)}, device_id_type=MESH)

    none = jnp.zeros((1, ROWS), f32)
    first = rem(y, 2) == 0
    me = c * NY + y
    rows2 = []
    for v in (w_in[...].astype(f32), t_in[...].astype(f32)):
        rows2.append(jnp.where(first, jnp.concatenate([v, none], 1), jnp.concatenate([none, v], 1)))
    wtb[me] = jnp.concatenate(rows2, 0)

    pl.semaphore_wait(barrier, len(yc_peers) + NX - 1 + NZ - 1)

    s0 = rem(x, 2) * 2
    s1 = s0 + 1
    o0 = 2 - s0
    o1 = o0 + 1
    up, down = at(y + 1, NY), at(y - 1, NY)
    far = at(y + 2, NY)
    right, left = at(x + 1, NX), at(x - 1, NX)
    MINUS, PLUS, FAR = 0, 1, 2
    load_own.wait()
    start(piece(c, y, s0), piece(c, y, s0), ra.at[MINUS * 4 + 0], y=up)
    start(piece(c, y, s1), piece(c, y, s1), ra.at[PLUS * 4 + 1], y=down)
    start(piece(c, y, s1), piece(c, y, s1), ra.at[MINUS * 4 + 1], y=up)
    start(piece(c, y, s0), piece(c, y, s0), ra.at[PLUS * 4 + 0], y=down)
    start(shard(c, y), shard(c, y), rd.at[12], c=1 - c)
    for k, (dy, dc) in enumerate(yc_peers):
        start(wtb.at[me], wtb.at[me], rw.at[k], y=at(y + dy, NY), c=at(c + dc, NC))

    where = {MINUS: down, PLUS: up, FAR: far}
    klass = (s0, s1, o0, o1)

    def got(src, k):
        p = piece(c, where[src], klass[k])
        arrived(p, ra.at[src * 4 + k])
        if k < 2 and src != FAR:
            if src == MINUS and k == 0:
                start(p, p, ra.at[FAR * 4 + 0], y=up)
            if src == PLUS and k == 1:
                start(p, p, ra.at[FAR * 4 + 1], y=down)
        if k == 0:
            start(p, p, ra.at[src * 4 + 2], x=left)
        if k == 1:
            start(p, p, ra.at[src * 4 + 3], x=right)
        start(p, p, rd.at[src * 4 + k], c=1 - c)

    def from_partner(k):
        for src in (MINUS, PLUS, FAR):
            arrived(piece(1 - c, where[src], klass[k]), rd.at[src * 4 + k])

    def add_logits(k, first_one):
        out = lax.dot_general(
            hid[:, cols(klass[k])], emb[:, cols(klass[k])], (((1,), (1,)), ((), ())), preferred_element_type=f32
        )
        logit[...] = out if first_one else logit[...] + out

    got(MINUS, 0)
    got(PLUS, 1)
    got(MINUS, 1)
    got(PLUS, 0)

    for k, (dy, dc) in enumerate(yc_peers):
        arrived(wtb.at[at(c - dc, NC) * NY + at(y - dy, NY)], rw.at[k])
    for b in range(TOKENS // 128):
        both = wtb[2 * b] + wtb[2 * b + 1]
        wrep[128 * b : 128 * b + 128, :] = jnp.broadcast_to(both[0:1, :], (128, 128)).T
        trep[128 * b : 128 * b + 128, :] = jnp.broadcast_to(both[1:2, :], (128, 128)).T

    got(MINUS, 2)
    got(PLUS, 3)
    got(FAR, 0)
    got(FAR, 1)
    for load in load_emb:
        load.wait()
    arrived(shard(1 - c, y), rd.at[12])
    got(PLUS, 2)
    got(MINUS, 3)
    from_partner(0)
    add_logits(0, True)
    got(FAR, 2)
    got(FAR, 3)
    from_partner(1)
    add_logits(1, False)
    from_partner(2)
    add_logits(2, False)
    from_partner(3)
    add_logits(3, False)

    def exps(i, carry):
        r = pl.ds(pl.multiple_of(i * 32, 32), 32)
        t = jnp.tanh(logit[r, :] * (1.0 / soft_cap))
        e = jnp.exp(soft_cap * t - soft_cap)
        logit[r, :] = e
        quad[r, :] = 1.0 - t * t
        total = e[:, 0:128]
        for k in range(1, VROWS // 128):
            total = total + e[:, 128 * k : 128 * k + 128]
        sums[r, :] = total
        return carry

    lax.fori_loop(0, TOKENS // 32, exps, 0)
    for b in range(TOKENS // 128):
        stat[0:1, 128 * b : 128 * b + 128] = jnp.sum(sums[128 * b : 128 * b + 128, :].T, axis=0, keepdims=True)

    for k, (dy, dc) in enumerate(yc_peers):
        start(stat, b1.at[k], rb.at[k], y=at(y + dy, NY), c=at(c + dc, NC))
    n1 = len(yc_peers)
    for k in range(n1):
        arrived(b1.at[k], rb.at[k])
    total = stat[...]
    for k in range(n1):
        total = total + b1[k]
    stat2[...] = total
    for d in range(1, NX):
        start(stat2, b2.at[d - 1], rb.at[n1 + d - 1], x=at(x + d, NX))
    for d in range(1, NX):
        arrived(b2.at[d - 1], rb.at[n1 + d - 1])
    for d in range(1, NX):
        total = total + b2[d - 1]
    stat3[...] = total
    n2 = n1 + NX - 1
    for d in range(1, NZ):
        start(stat3, b3.at[d - 1], rb.at[n2 + d - 1], z=at(z + d, NZ))
    for d in range(1, NZ):
        arrived(b3.at[d - 1], rb.at[n2 + d - 1])
    for d in range(1, NZ):
        total = total + b3[d - 1]
    rate = (1.0 + 2.0 * z_weight * (soft_cap + jnp.log(total))) / total
    for b in range(TOKENS // 128):
        frep[128 * b : 128 * b + 128, :] = jnp.broadcast_to(rate[0:1, 128 * b : 128 * b + 128], (128, 128)).T

    base = ((((y * NC + c) * NX + x) * NZ + z) * VROWS).astype(f32)

    def scores(i, carry):
        r = pl.ds(pl.multiple_of(i * 32, 32), 32)
        w = wrep[r, :]
        fac = frep[r, :] * w
        want = trep[r, :] - base
        lane = lax.broadcasted_iota(jnp.int32, (32, 128), 1).astype(f32)
        for k in range(VROWS // 128):
            s = slice(128 * k, 128 * k + 128)
            hit = jnp.where(want == lane + float(128 * k), w, 0.0)
            sc[r, s] = ((fac * logit[r, s] - hit) * quad[r, s]).astype(bf16)
        return carry

    lax.fori_loop(0, TOKENS // 32, scores, 0)

    other_rows = pl.ds(pl.multiple_of((1 - c) * HALF, HALF), HALF)
    own_rows = pl.ds(pl.multiple_of(c * HALF, HALF), HALF)
    blocks = [at(x + d, NX) for d in ORDER]
    for i in range(NX):
        e = emb[:, cols(blocks[i])]
        dsend[i] = jnp.dot(sc[other_rows, :], e, preferred_element_type=f32).astype(bf16)
        start(dsend.at[i], drecv.at[i], rdd.at[i], c=1 - c)
        own[i] = jnp.dot(sc[own_rows, :], e, preferred_element_type=f32)
    for i, d in enumerate(ORDER):
        arrived(drecv.at[i], rdd.at[i])
        chip = own[i] + drecv[i].astype(f32)
        own[i] = chip
        xs[i] = chip.astype(bf16).reshape(NY, 2, SUB, BLK)
        for dy in (2, 1, 3):
            yy = at(y + dy, NY)
            start(xs.at[i, yy, 0], ry.at[dy - 1, i], rsy.at[(dy - 1) * NX + i], y=yy)
        if d:
            start(xs.at[i, :, 1], rx.at[d - 1], rsx.at[d - 1], x=blocks[i])

    for k in range(VROWS // 128):
        s = slice(128 * k, 128 * k + 128)
        sct[s, :] = sc[:, s].astype(f32).T.astype(bf16)
    outs = []
    for i in range(NX):
        stage[i] = jnp.dot(sct[...], hid[:, i * BLK : (i + 1) * BLK], preferred_element_type=f32).astype(bf16)
        outs.append(pltpu.make_async_copy(stage.at[i], tg_out.at[:, i * BLK : (i + 1) * BLK], tg_sem.at[i]))
        outs[-1].start()

    def own_part(i, yy, colour):
        return own[i, pl.ds(pl.multiple_of(yy * ROWS + colour * SUB, SUB), SUB), :]

    for i, d in enumerate(ORDER):
        total = own_part(i, y, 0)
        for dy in range(1, NY):
            arrived(ry.at[dy - 1, i], rsy.at[(dy - 1) * NX + i])
            total = total + ry[dy - 1, i].astype(f32)
        if d:
            ys[d - 1] = total.astype(bf16)
            start(ys.at[d - 1], sy.at[d - 1], rty.at[d - 1], x=blocks[i])
        else:
            keep0 = total
    for d in range(1, NX):
        arrived(rx.at[d - 1], rsx.at[d - 1])
    mine = ORDER.index(0)

    def x_sum(yy):
        total = own_part(mine, yy, 1)
        for d in range(1, NX):
            total = total + rx[d - 1, yy].astype(f32)
        return total

    for dy in (2, 1, 3):
        yy = at(y + dy, NY)
        xs2[dy - 1] = x_sum(yy).astype(bf16)
        start(xs2.at[dy - 1], sx.at[dy - 1], rtx.at[dy - 1], y=yy)
    keep1 = x_sum(y)
    for d in range(1, NX):
        arrived(sy.at[d - 1], rty.at[d - 1])
        keep0 = keep0 + sy[d - 1].astype(f32)
    for d in range(1, NY):
        arrived(sx.at[d - 1], rtx.at[d - 1])
        keep1 = keep1 + sx[d - 1].astype(f32)

    half = NZ // 2
    zs[0:half] = keep0.reshape(half, ZR, BLK)
    zs[half:NZ] = keep1.reshape(half, ZR, BLK)
    for d in (4, 3, 5, 2, 6, 1, 7):
        zz = at(z + d, NZ)
        start(zs.at[zz], rz.at[d - 1], rzs.at[d - 1], z=zz)
    total = zs[z]
    for d in range(1, NZ):
        arrived(rz.at[d - 1], rzs.at[d - 1])
        total = total + rz[d - 1]
    gz[z] = total.astype(bf16)
    for d in (4, 3, 5, 2, 6, 1, 7):
        start(gz.at[z], gz.at[z], rzg.at[d - 1], z=at(z + d, NZ))
    for d in range(1, NZ):
        arrived(gz.at[at(z - d, NZ)], rzg.at[d - 1])
    for d in (2, 1, 3):
        start(gz, gx.at[d - 1], rxg.at[d - 1], x=at(x + d, NX))
    hg_out[:, cols(x)] = gz[...].reshape(ROWS, BLK)
    for d in range(1, NX):
        arrived(gx.at[d - 1], rxg.at[d - 1])
        hg_out[:, cols(at(x - d, NX))] = gx[d - 1].reshape(ROWS, BLK)

    for out in outs:
        out.wait()
    for copy in sends:
        copy.wait_send()


def body(hidden, embedding, targets, loss_weight):
    vm = pltpu.VMEM
    dma = pltpu.SemaphoreType.DMA
    return pl.pallas_call(
        kernel,
        out_shape=(
            jax.ShapeDtypeStruct((ROWS, D), bf16),
            jax.ShapeDtypeStruct((VROWS, D), bf16),
        ),
        in_specs=[
            pl.BlockSpec(memory_space=pl.ANY),
            pl.BlockSpec(memory_space=pl.ANY),
            pl.BlockSpec(memory_space=pltpu.VMEM),
            pl.BlockSpec(memory_space=pltpu.VMEM),
        ],
        out_specs=(pl.BlockSpec(memory_space=pltpu.VMEM), pl.BlockSpec(memory_space=pl.ANY)),
        scratch_shapes=[
            vm((TOKENS, D), bf16),
            vm((VROWS, D), bf16),
            vm((NC * NY, 2, 128), f32),
            vm((TOKENS, 128), f32),
            vm((TOKENS, 128), f32),
            vm((TOKENS, VROWS), f32),
            vm((TOKENS, VROWS), f32),
            vm((TOKENS, 128), f32),
            vm((1, TOKENS), f32),
            vm((1, TOKENS), f32),
            vm((1, TOKENS), f32),
            vm((TOKENS, 128), f32),
            vm((NY * NC - 1, 1, TOKENS), f32),
            vm((NX - 1, 1, TOKENS), f32),
            vm((NZ - 1, 1, TOKENS), f32),
            vm((TOKENS, VROWS), bf16),
            vm((VROWS, TOKENS), bf16),
            vm((NX, HALF, BLK), f32),
            vm((NX, HALF, BLK), bf16),
            vm((NX, HALF, BLK), bf16),
            vm((NX, NY, 2, SUB, BLK), bf16),
            vm((NY - 1, NX, SUB, BLK), bf16),
            vm((NX - 1, NY, SUB, BLK), bf16),
            vm((NX - 1, SUB, BLK), bf16),
            vm((NY - 1, SUB, BLK), bf16),
            vm((NX - 1, SUB, BLK), bf16),
            vm((NY - 1, SUB, BLK), bf16),
            vm((NZ, ZR, BLK), f32),
            vm((NZ - 1, ZR, BLK), f32),
            vm((NZ, ZR, BLK), bf16),
            vm((NX - 1, NZ, ZR, BLK), bf16),
            vm((NX, VROWS, BLK), bf16),
            dma((1 + NX,)),
            dma((104,)),
            dma((12,)),
            dma((13,)),
            dma((NY * NC - 1,)),
            dma((NY * NC + NX + NZ - 3,)),
            dma((NX,)),
            dma(((NY - 1) * NX,)),
            dma((NX - 1,)),
            dma((NX - 1,)),
            dma((NY - 1,)),
            dma((NZ - 1,)),
            dma((NZ - 1,)),
            dma((NX - 1,)),
            dma((NX,)),
        ],
        compiler_params=pltpu.CompilerParams(collective_id=0, has_side_effects=True, vmem_limit_bytes=60 * 1024 * 1024),
        name="head_backward",
    )(hidden, embedding, loss_weight.reshape(1, ROWS), targets.reshape(1, ROWS))


def solution(mesh):
    finer = Mesh(mesh.devices.reshape(NY, NC, NX, NZ), ("y", "c", "x", "z"))
    dp = ("y", "c")
    both = ("y", "c", "x", "z")
    return jax.shard_map(
        body,
        mesh=finer,
        in_specs=(P(dp, None), P(both, None), P(dp), P(dp)),
        out_specs=(P(dp, None), P(both, None)),
        check_vma=False,
    )
```

time: 272 us -> 91.4 us (0.34)
  blocking collectives: 176 us -> 0 us
  Pallas kernels: 0 us -> 82.4 us
  waiting for transfers between devices: 36.5 us -> 0 us
  matrix products: 22.8 us -> 0 us
  between operations: 14.1 us -> 0.64 us
  starting transfers between devices: 12.1 us -> 0 us
  other arithmetic: 3.52 us -> 0 us
    unnamed x1 -> x0, blocking collectives: 139 us -> none
    pallas_call x0 -> x1, Pallas kernels: none -> 82.4 us  [body(): pl.pallas_call(kernel, out_shape=(jax.ShapeDtypeStruct((ROWS, D), bf16),...]
    psum x4 -> x0, blocking collectives: 37.1 us -> none  [over_axes(): x = lax.psum(x, axis)]
    all_gather x1 -> x0, waiting for transfers between devices: 24.3 us -> none  [in_one_piece(): result, at, outs = (lax.all_gather(both, axis, axis=dim, tiled=True), 0, [])]
    dot_general x3 -> x0, matrix products: 22.8 us -> none  [the longest x1 8.06 us: body(): jnp.dot(scores_grad, embedding, preferred_element_type=jnp.float32)]
    all_to_all x2 -> x0, waiting for transfers between devices: 12.1 us -> none  [from_everyone(): return lax.all_to_all(copies, axis, split_axis=0, concat_axis=0, tiled=True)]
    all_to_all x2 -> x0, starting transfers between devices: 12.1 us -> none  [from_everyone(): return lax.all_to_all(copies, axis, split_axis=0, concat_axis=0, tiled=True)]
    unnamed x0 -> x2, local copies, waits for them, and re-layouts: none -> 7.17 us
  transfers between devices with their start and end apart: 3 -> 0, of which waited for: 3 -> 0; matrix products, arithmetic and copies ran while one was open for 4% -> 0% of each run, Pallas kernels for 0% -> 0%
where the time goes in v1:
time: 91.4 us; the launch traced here: 90.2 us
  Pallas kernels  82.4 us (90%)
  local copies, waits for them, and re-layouts  7.17 us (8%)
    pallas_call x1, Pallas kernels, body(): pl.pallas_call(kernel, out_shape=(jax.ShapeDtypeStruct((ROWS, D), bf16),...  82.4 us
    unnamed x2, local copies, waits for them, and re-layouts  7.17 us

profile of v1, /device:TPU:2, one launch (start us, length us, event | category | flops | bytes accessed | tf_op | source)
XLA Modules:
  0.0 90.2 jit_solution(12959836587125431857)
XLA Ops:
  0.6 82.4 %head_backward.1 = (bf16[64,3584]{1,0:T(8,128)(2,1)}, bf16[768,3584]{1,0:T(8,128)(2,1)}) custom-call(bf16[64,3584]{1,0:T(8,128)(2,1)} %hid_in.1, bf16[768,3584]{1,0:T(8,128)(2,1)} %emb_in.1, bf16[1,64]{1,0:T(2,128)(2,1)} %bitcast.2, s32[1,64]{1,0:T(1,128)} %bitcast.3), custom_call_target="tpu_custom_call" | custom-call | tf_op jit(solution)/shard_map/head_backward/pallas_call | solution.py:318
  83.0 1.8 %copy.8 = bf16[64,3584]{1,0:T(8,128)(2,1)} copy(bf16[64,3584]{1,0:T(8,128)(2,1)} %get-tuple-element.4) | data formatting | bytes 917504
  84.9 5.4 %copy.9 = bf16[768,3584]{1,0:T(8,128)(2,1)} copy(bf16[768,3584]{1,0:T(8,128)(2,1)} %get-tuple-element.5) | data formatting | bytes 11010048

commit v2 on v1

--- a/solution.py
+++ b/solution.py
@@ -26,9 +26,9 @@
 
 def kernel(
     hid_in, emb_in, w_in, t_in, hg_out, tg_out,
-    hid, emb, wtb, wrep, trep, logit, quad, sums, stat, stat2, stat3, frep, b1, b2, b3,
-    sc, sct, own, dsend, drecv, xs, ry, rx, ys, xs2, sy, sx, zs, rz, gz, gx, stage,
-    local_sem, send_sem, ra, rd, rw, rb, rdd, rsy, rsx, rty, rtx, rzs, rzg, rxg, tg_sem,
+    w_own, t_own, hid, emb, wtb, wrep, trep, logit, quad, sums, stat, stat2, stat3, frep, b1, b2, b3,
+    sc, sct, own, dsend, drecv, xs, ry, rx, ys, xs2, sy, sx, zf, zs, rz, gz, gx,
+    local_sem, send_sem, ra, rd, rw, rb, rdd, rsy, rsx, rty, rtx, rzs, rzg, rxg,
 ):
     y, c, x, z = (lax.axis_index(a) for a in ("y", "c", "x", "z"))
     rem = lax.rem
@@ -50,22 +50,29 @@
             src_ref=dst, dst_ref=dst, send_sem=send_sem.at[0], recv_sem=rsem, device_id={"c": 1 - c}, device_id_type=MESH
         ).wait_recv()
 
+    me = c * NY + y
+
     def cols(q):
         return pl.ds(pl.multiple_of(q * BLK, 128), BLK)
 
-    def piece(cc, yy, q):
-        return hid.at[pl.ds(pl.multiple_of((cc * NY + yy) * ROWS, ROWS), ROWS), cols(q)]
-
     def shard(cc, yy):
         return hid.at[pl.ds(pl.multiple_of((cc * NY + yy) * ROWS, ROWS), ROWS)]
 
-    load_own = pltpu.make_async_copy(hid_in, shard(c, y), local_sem.at[0])
-    load_own.start()
+    def piece(cc, yy, q, lo, hi):
+        rows = pl.ds(pl.multiple_of((cc * NY + yy) * ROWS, ROWS), ROWS)
+        return hid.at[rows, pl.ds(pl.multiple_of(q * BLK + lo, 128), hi - lo)]
+
+    load_own = [
+        pltpu.make_async_copy(hid_in, shard(c, y), local_sem.at[NX]),
+        pltpu.make_async_copy(w_in, w_own, local_sem.at[NX + 1]),
+        pltpu.make_async_copy(t_in, t_own, local_sem.at[NX + 2]),
+    ]
     load_emb = []
     for k in range(NX):
         part = pl.ds(k * (VROWS // NX), VROWS // NX)
-        load_emb.append(pltpu.make_async_copy(emb_in.at[part], emb.at[part], local_sem.at[1 + k]))
-        load_emb[-1].start()
+        load_emb.append(pltpu.make_async_copy(emb_in.at[part], emb.at[part], local_sem.at[k]))
+    for load in load_own + load_emb:
+        load.start()
 
     barrier = pltpu.get_barrier_semaphore()
     yc_peers = [(dy, dc) for dy in range(NY) for dc in range(NC) if (dy, dc) != (0, 0)]
@@ -76,64 +83,73 @@
     for d in range(1, NZ):
         pl.semaphore_signal(barrier, inc=1, device_id={"z": at(z + d, NZ)}, device_id_type=MESH)
 
+    for load in load_own:
+        load.wait()
     none = jnp.zeros((1, ROWS), f32)
     first = rem(y, 2) == 0
-    me = c * NY + y
     rows2 = []
-    for v in (w_in[...].astype(f32), t_in[...].astype(f32)):
+    for v in (w_own[...].astype(f32), t_own[...].astype(f32)):
         rows2.append(jnp.where(first, jnp.concatenate([v, none], 1), jnp.concatenate([none, v], 1)))
     wtb[me] = jnp.concatenate(rows2, 0)
 
     pl.semaphore_wait(barrier, len(yc_peers) + NX - 1 + NZ - 1)
 
-    s0 = rem(x, 2) * 2
-    s1 = s0 + 1
-    o0 = 2 - s0
-    o1 = o0 + 1
-    up, down = at(y + 1, NY), at(y - 1, NY)
-    far = at(y + 2, NY)
+    k0 = rem(x + 2 * z, NX)
+    kp, km, k2 = rem(k0 + 1, NX), rem(k0 + 3, NX), rem(k0 + 2, NX)
+    up, down, far = at(y + 1, NY), at(y - 1, NY), at(y + 2, NY)
     right, left = at(x + 1, NX), at(x - 1, NX)
+    above, below = at(z + 1, NZ), at(z - 1, NZ)
     MINUS, PLUS, FAR = 0, 1, 2
-    load_own.wait()
-    start(piece(c, y, s0), piece(c, y, s0), ra.at[MINUS * 4 + 0], y=up)
-    start(piece(c, y, s1), piece(c, y, s1), ra.at[PLUS * 4 + 1], y=down)
-    start(piece(c, y, s1), piece(c, y, s1), ra.at[MINUS * 4 + 1], y=up)
-    start(piece(c, y, s0), piece(c, y, s0), ra.at[PLUS * 4 + 0], y=down)
-    start(shard(c, y), shard(c, y), rd.at[12], c=1 - c)
+    where = {MINUS: down, PLUS: up, FAR: far}
+    P1, P2, P3, P4, R1, R2, L1, L2, ZU, ZD = range(10)
+    parts = (
+        (k0, 0, 512), (k0, 512, BLK), (kp, 0, 256), (km, 0, 256),
+        (kp, 256, 512), (kp, 512, BLK), (km, 256, 512), (km, 512, BLK),
+        (k2, 0, 512), (k2, 512, BLK),
+    )
+    NP = len(parts)
+
+    def own_to(p, src, yy):
+        part = piece(c, y, *parts[p])
+        start(part, part, ra.at[src * NP + p], y=yy)
+
+    for p, q in ((P1, P2), (P3, P4), (P2, P1), (P4, P3)):
+        own_to(p, MINUS, up)
+        own_to(q, PLUS, down)
+    start(shard(c, y), shard(c, y), rd.at[3 * NP], c=1 - c)
     for k, (dy, dc) in enumerate(yc_peers):
         start(wtb.at[me], wtb.at[me], rw.at[k], y=at(y + dy, NY), c=at(c + dc, NC))
 
-    where = {MINUS: down, PLUS: up, FAR: far}
-    klass = (s0, s1, o0, o1)
-
-    def got(src, k):
-        p = piece(c, where[src], klass[k])
-        arrived(p, ra.at[src * 4 + k])
-        if k < 2 and src != FAR:
-            if src == MINUS and k == 0:
-                start(p, p, ra.at[FAR * 4 + 0], y=up)
-            if src == PLUS and k == 1:
-                start(p, p, ra.at[FAR * 4 + 1], y=down)
-        if k == 0:
-            start(p, p, ra.at[src * 4 + 2], x=left)
-        if k == 1:
-            start(p, p, ra.at[src * 4 + 3], x=right)
-        start(p, p, rd.at[src * 4 + k], c=1 - c)
-
-    def from_partner(k):
-        for src in (MINUS, PLUS, FAR):
-            arrived(piece(1 - c, where[src], klass[k]), rd.at[src * 4 + k])
-
-    def add_logits(k, first_one):
+    def got(src, p):
+        part = piece(c, where[src], *parts[p])
+        arrived(part, ra.at[src * NP + p])
+        if src == MINUS and p in (P1, P3):
+            start(part, part, ra.at[FAR * NP + p], y=up)
+        if src == PLUS and p in (P2, P4):
+            start(part, part, ra.at[FAR * NP + p], y=down)
+        if p in (P1, P2):
+            sub = piece(c, where[src], k0, 256, 512) if p == P1 else part
+            start(sub, sub, ra.at[src * NP + (R1 if p == P1 else R2)], x=left)
+            start(sub, sub, ra.at[src * NP + (L1 if p == P1 else L2)], x=right)
+            if p == P1:
+                start(part, part, ra.at[src * NP + ZU], z=below)
+            else:
+                start(part, part, ra.at[src * NP + ZD], z=above)
+        start(part, part, rd.at[src * NP + p], c=1 - c)
+
+    def from_partner(*ps):
+        for p in ps:
+            for src in (MINUS, PLUS, FAR):
+                arrived(piece(1 - c, where[src], *parts[p]), rd.at[src * NP + p])
+
+    def add_logits(q, first_one):
         out = lax.dot_general(
-            hid[:, cols(klass[k])], emb[:, cols(klass[k])], (((1,), (1,)), ((), ())), preferred_element_type=f32
+            hid[:, cols(q)], emb[:, cols(q)], (((1,), (1,)), ((), ())), preferred_element_type=f32
         )
         logit[...] = out if first_one else logit[...] + out
 
-    got(MINUS, 0)
-    got(PLUS, 1)
-    got(MINUS, 1)
-    got(PLUS, 0)
+    for src, p in ((PLUS, P2), (MINUS, P1), (PLUS, P4), (MINUS, P3), (MINUS, P2), (PLUS, P1)):
+        got(src, p)
 
     for k, (dy, dc) in enumerate(yc_peers):
         arrived(wtb.at[at(c - dc, NC) * NY + at(y - dy, NY)], rw.at[k])
@@ -142,25 +158,25 @@
         wrep[128 * b : 128 * b + 128, :] = jnp.broadcast_to(both[0:1, :], (128, 128)).T
         trep[128 * b : 128 * b + 128, :] = jnp.broadcast_to(both[1:2, :], (128, 128)).T
 
-    got(MINUS, 2)
-    got(PLUS, 3)
-    got(FAR, 0)
-    got(FAR, 1)
+    for src, p in (
+        (MINUS, P4), (PLUS, P3), (PLUS, R2), (PLUS, L2), (PLUS, ZD), (MINUS, R1), (MINUS, L1), (MINUS, ZU),
+        (FAR, P2), (FAR, P1), (FAR, P4), (FAR, P3), (MINUS, R2), (MINUS, L2), (MINUS, ZD), (PLUS, ZU),
+        (PLUS, R1), (PLUS, L1),
+    ):
+        got(src, p)
     for load in load_emb:
         load.wait()
-    arrived(shard(1 - c, y), rd.at[12])
-    got(PLUS, 2)
-    got(MINUS, 3)
-    from_partner(0)
-    add_logits(0, True)
-    got(FAR, 2)
-    got(FAR, 3)
-    from_partner(1)
-    add_logits(1, False)
-    from_partner(2)
-    add_logits(2, False)
-    from_partner(3)
-    add_logits(3, False)
+    arrived(shard(1 - c, y), rd.at[3 * NP])
+    from_partner(P1, P2)
+    add_logits(k0, True)
+    for p in (R2, L2, ZD, R1, L1, ZU):
+        got(FAR, p)
+    from_partner(P3, R2, R1)
+    add_logits(kp, False)
+    from_partner(P4, L2, L1)
+    add_logits(km, False)
+    from_partner(ZD, ZU)
+    add_logits(k2, False)
 
     def exps(i, carry):
         r = pl.ds(pl.multiple_of(i * 32, 32), 32)
@@ -243,11 +259,10 @@
     for k in range(VROWS // 128):
         s = slice(128 * k, 128 * k + 128)
         sct[s, :] = sc[:, s].astype(f32).T.astype(bf16)
-    outs = []
     for i in range(NX):
-        stage[i] = jnp.dot(sct[...], hid[:, i * BLK : (i + 1) * BLK], preferred_element_type=f32).astype(bf16)
-        outs.append(pltpu.make_async_copy(stage.at[i], tg_out.at[:, i * BLK : (i + 1) * BLK], tg_sem.at[i]))
-        outs[-1].start()
+        tg_out[:, i * BLK : (i + 1) * BLK] = jnp.dot(
+            sct[...], hid[:, i * BLK : (i + 1) * BLK], preferred_element_type=f32
+        ).astype(bf16)
 
     def own_part(i, yy, colour):
         return own[i, pl.ds(pl.multiple_of(yy * ROWS + colour * SUB, SUB), SUB), :]
@@ -285,29 +300,34 @@
         keep1 = keep1 + sx[d - 1].astype(f32)
 
     half = NZ // 2
-    zs[0:half] = keep0.reshape(half, ZR, BLK)
-    zs[half:NZ] = keep1.reshape(half, ZR, BLK)
+    zf[0:half] = keep0.reshape(half, ZR, BLK)
+    zf[half:NZ] = keep1.reshape(half, ZR, BLK)
+    zs[...] = zf[...].astype(bf16)
     for d in (4, 3, 5, 2, 6, 1, 7):
         zz = at(z + d, NZ)
         start(zs.at[zz], rz.at[d - 1], rzs.at[d - 1], z=zz)
-    total = zs[z]
-    for d in range(1, NZ):
+    total = zf[z]
+    for d in (1, 7, 2, 6, 3, 5, 4):
         arrived(rz.at[d - 1], rzs.at[d - 1])
-        total = total + rz[d - 1]
+        total = total + rz[d - 1].astype(f32)
     gz[z] = total.astype(bf16)
     for d in (4, 3, 5, 2, 6, 1, 7):
         start(gz.at[z], gz.at[z], rzg.at[d - 1], z=at(z + d, NZ))
-    for d in range(1, NZ):
+
+    def on_to_x(d, zz):
+        for dx in (2, 1, 3):
+            start(gz.at[zz], gx.at[dx - 1, zz], rxg.at[(dx - 1) * NZ + d], x=at(x + dx, NX))
+
+    on_to_x(0, z)
+    for d in (1, 7, 2, 6, 3, 5, 4):
         arrived(gz.at[at(z - d, NZ)], rzg.at[d - 1])
-    for d in (2, 1, 3):
-        start(gz, gx.at[d - 1], rxg.at[d - 1], x=at(x + d, NX))
+        on_to_x(d, at(z - d, NZ))
     hg_out[:, cols(x)] = gz[...].reshape(ROWS, BLK)
-    for d in range(1, NX):
-        arrived(gx.at[d - 1], rxg.at[d - 1])
-        hg_out[:, cols(at(x - d, NX))] = gx[d - 1].reshape(ROWS, BLK)
-
-    for out in outs:
-        out.wait()
+    for dx in range(1, NX):
+        for d in range(NZ):
+            arrived(gx.at[dx - 1, at(z - d, NZ)], rxg.at[(dx - 1) * NZ + d])
+        hg_out[:, cols(at(x - dx, NX))] = gx[dx - 1].reshape(ROWS, BLK)
+
     for copy in sends:
         copy.wait_send()
 
@@ -324,11 +344,13 @@
         in_specs=[
             pl.BlockSpec(memory_space=pl.ANY),
             pl.BlockSpec(memory_space=pl.ANY),
-            pl.BlockSpec(memory_space=pltpu.VMEM),
-            pl.BlockSpec(memory_space=pltpu.VMEM),
+            pl.BlockSpec(memory_space=pl.ANY),
+            pl.BlockSpec(memory_space=pl.ANY),
         ],
-        out_specs=(pl.BlockSpec(memory_space=pltpu.VMEM), pl.BlockSpec(memory_space=pl.ANY)),
+        out_specs=(pl.BlockSpec(memory_space=pltpu.VMEM), pl.BlockSpec(memory_space=pltpu.VMEM)),
         scratch_shapes=[
+            vm((1, ROWS), bf16),
+            vm((1, ROWS), jnp.int32),
             vm((TOKENS, D), bf16),
             vm((VROWS, D), bf16),
             vm((NC * NY, 2, 128), f32),
@@ -357,14 +379,14 @@
             vm((NX - 1, SUB, BLK), bf16),
             vm((NY - 1, SUB, BLK), bf16),
             vm((NZ, ZR, BLK), f32),
-            vm((NZ - 1, ZR, BLK), f32),
+            vm((NZ, ZR, BLK), bf16),
+            vm((NZ - 1, ZR, BLK), bf16),
             vm((NZ, ZR, BLK), bf16),
             vm((NX - 1, NZ, ZR, BLK), bf16),
-            vm((NX, VROWS, BLK), bf16),
-            dma((1 + NX,)),
-            dma((104,)),
-            dma((12,)),
-            dma((13,)),
+            dma((NX + 3,)),
+            dma((160,)),
+            dma((30,)),
+            dma((31,)),
             dma((NY * NC - 1,)),
             dma((NY * NC + NX + NZ - 3,)),
             dma((NX,)),
@@ -374,12 +396,11 @@
             dma((NY - 1,)),
             dma((NZ - 1,)),
             dma((NZ - 1,)),
-            dma((NX - 1,)),
-            dma((NX,)),
+            dma(((NX - 1) * NZ,)),
         ],
-        compiler_params=pltpu.CompilerParams(collective_id=0, has_side_effects=True, vmem_limit_bytes=60 * 1024 * 1024),
+        compiler_params=pltpu.CompilerParams(collective_id=0, has_side_effects=True, vmem_limit_bytes=44 * 1024 * 1024),
         name="head_backward",
-    )(hidden, embedding, loss_weight.reshape(1, ROWS), targets.reshape(1, ROWS))
+    )(*(pltpu.with_memory_space_constraint(a, pltpu.HBM) for a in (hidden, embedding, loss_weight.reshape(1, ROWS), targets.reshape(1, ROWS))))
 
 
 def solution(mesh):

time: 91.4 us -> 80.4 us (0.88); the launches traced: 90.2 us -> 80.3 us
  Pallas kernels: 82.4 us -> 76.5 us
  local copies, waits for them, and re-layouts: 7.17 us -> 3.21 us
    pallas_call x1, Pallas kernels: 82.4 us -> 76.5 us  [body(): pl.pallas_call(kernel, out_shape=(jax.ShapeDtypeStruct((ROWS, D), bf16),...]
    unnamed x2, local copies, waits for them, and re-layouts: 7.17 us -> 3.21 us
where the time goes in v2:
time: 80.4 us; the launch traced here: 80.3 us
  Pallas kernels  76.5 us (95%)
  local copies, waits for them, and re-layouts  3.21 us (4%)
    pallas_call x1, Pallas kernels, body(): pl.pallas_call(kernel, out_shape=(jax.ShapeDtypeStruct((ROWS, D), bf16),...  76.5 us
    unnamed x2, local copies, waits for them, and re-layouts  3.21 us

profile of v2, /device:TPU:2, one launch (start us, length us, event | category | flops | bytes accessed | tf_op | source)
XLA Modules:
  0.0 80.3 jit_solution(17743621821696717857)
XLA Ops:
  0.6 76.5 %head_backward.1 = (bf16[64,3584]{1,0:T(8,128)(2,1)S(1)}, bf16[768,3584]{1,0:T(8,128)(2,1)S(1)}) custom-call(bf16[64,3584]{1,0:T(8,128)(2,1)} %hid_in.1, bf16[768,3584]{1,0:T(8,128)(2,1)} %emb_in.1, bf16[1,64]{1,0:T(2,128)(2,1)} %bitcast.2, s32[1,64]{1,0:T(1,128)} %bitcast.3), custom_call_target="tpu_custom_call" | custom-call | tf_op jit(solution)/shard_map/head_backward/pallas_call | solution.py:338
  77.1 0.8 copy.8
  77.9 2.4 %copy.9 = bf16[768,3584]{1,0:T(8,128)(2,1)} copy(bf16[768,3584]{1,0:T(8,128)(2,1)S(1)} %get-tuple-element.5) | data formatting | bytes 11010048

commit v3 on v2

v3 whole, which is shorter than its diff:
```python
import functools

import jax
import jax.numpy as jnp
from jax import lax
from jax.experimental import pallas as pl
from jax.experimental.pallas import tpu as pltpu
from jax.sharding import Mesh
from jax.sharding import PartitionSpec as P

MESH = pl.DeviceIdType.MESH
f32, bf16 = jnp.float32, jnp.bfloat16

NY, NC, NX, NZ = 4, 2, 4, 8
D, VROWS, ROWS = 3584, 768, 64
TOKENS = ROWS * NY * NC
HALF = ROWS * NY
BLK = D // NX
SUB = ROWS // 2
ZR = ROWS // NZ
ORDER = (2, 1, 3, 0)

soft_cap = 30.0
z_weight = 0.002


def kernel(
    hid_in, emb_in, w_in, t_in, hg_out, tg_out,
    w_own, t_own, hid, emb, wtb, wrep, trep, prob, sums, hits, stat, stat2, stat3, rate, frep, grep, b1, b2, b3,
    pm, hm, sc, sct, own, town, asend, arecv, tsend, trecv, fy, fyr, ny, nyr, fx, fxr, nx, nxr,
    ys, xs2, sy, sx, zf, zs, rz, gz, gx,
    local_sem, send_sem, ra, rd, rw, rb, rda, rdt, rfy, rny, rfx, rnx, rty, rtx, rzs, rzg, rxg,
):
    y, c, x, z = (lax.axis_index(a) for a in ("y", "c", "x", "z"))
    rem = lax.rem

    def at(i, n):
        return rem(i + n, n)

    up, down, far = at(y + 1, NY), at(y - 1, NY), at(y + 2, NY)
    right, left = at(x + 1, NX), at(x - 1, NX)
    above, below = at(z + 1, NZ), at(z - 1, NZ)
    OWN, PLUS, MINUS, FAR = range(4)
    where = {OWN: y, PLUS: up, MINUS: down, FAR: far}
    RHO = ((0, OWN), (0, PLUS), (0, MINUS), (0, FAR), (1, FAR), (1, OWN), (1, PLUS), (1, MINUS))
    row_of = {key: ROWS * k for k, key in enumerate(RHO)}
    me = c * NY + y

    def group(e, s):
        return (1 - c if e else c) * NY + where[s]

    sends = []

    def start(src, dst, rsem, **dev):
        copy = pltpu.make_async_remote_copy(
            src_ref=src, dst_ref=dst, send_sem=send_sem.at[len(sends)], recv_sem=rsem, device_id=dev, device_id_type=MESH
        )
        copy.start()
        sends.append(copy)

    def arrived(dst, rsem):
        pltpu.make_async_remote_copy(
            src_ref=dst, dst_ref=dst, send_sem=send_sem.at[0], recv_sem=rsem, device_id={"c": 1 - c}, device_id_type=MESH
        ).wait_recv()

    def cols(q):
        return pl.ds(pl.multiple_of(q * BLK, 128), BLK)

    def shard(e, s):
        return hid.at[row_of[e, s] : row_of[e, s] + ROWS]

    def piece(e, s, q, lo, hi):
        return hid.at[row_of[e, s] : row_of[e, s] + ROWS, pl.ds(pl.multiple_of(q * BLK + lo, 128), hi - lo)]

    load_own = [
        pltpu.make_async_copy(hid_in, shard(0, OWN), local_sem.at[NX]),
        pltpu.make_async_copy(w_in, w_own, local_sem.at[NX + 1]),
        pltpu.make_async_copy(t_in, t_own, local_sem.at[NX + 2]),
    ]
    load_emb = []
    for k in range(NX):
        part = pl.ds(k * (VROWS // NX), VROWS // NX)
        load_emb.append(pltpu.make_async_copy(emb_in.at[part], emb.at[part], local_sem.at[k]))
    for load in load_own + load_emb:
        load.start()

    barrier = pltpu.get_barrier_semaphore()
    yc_peers = [(dy, dc) for dy in range(NY) for dc in range(NC) if (dy, dc) != (0, 0)]
    for dy, dc in yc_peers:
        pl.semaphore_signal(barrier, inc=1, device_id={"y": at(y + dy, NY), "c": at(c + dc, NC)}, device_id_type=MESH)
    for d in range(1, NX):
        pl.semaphore_signal(barrier, inc=1, device_id={"x": at(x + d, NX)}, device_id_type=MESH)
    for d in range(1, NZ):
        pl.semaphore_signal(barrier, inc=1, device_id={"z": at(z + d, NZ)}, device_id_type=MESH)

    for load in load_own:
        load.wait()
    none = jnp.zeros((1, ROWS), f32)
    wtb[me] = jnp.concatenate(
        [jnp.concatenate([v, none], 1) for v in (w_own[...].astype(f32), t_own[...].astype(f32))], 0
    )

    pl.semaphore_wait(barrier, len(yc_peers) + NX - 1 + NZ - 1)

    k0 = rem(x + 2 * z, NX)
    kp, km, k2 = rem(k0 + 1, NX), rem(k0 + 3, NX), rem(k0 + 2, NX)
    P1, P2, P3, P4, R1, R2, L1, L2, ZU, ZD = range(10)
    parts = (
        (k0, 0, 512), (k0, 512, BLK), (kp, 0, 256), (km, 0, 256),
        (kp, 256, 512), (kp, 512, BLK), (km, 256, 512), (km, 512, BLK),
        (k2, 0, 512), (k2, 512, BLK),
    )
    NP = len(parts)

    def slot(s, p):
        return (s - 1) * NP + p

    def to_up(s, p):
        start(piece(0, s, *parts[p]), piece(0, MINUS if s == OWN else FAR, *parts[p]), ra.at[slot(MINUS if s == OWN else FAR, p)], y=up)

    def to_down(s, p):
        start(piece(0, s, *parts[p]), piece(0, PLUS if s == OWN else FAR, *parts[p]), ra.at[slot(PLUS if s == OWN else FAR, p)], y=down)

    for p, q in ((P1, P2), (P3, P4), (P2, P1), (P4, P3)):
        to_up(OWN, p)
        to_down(OWN, q)
    start(shard(0, OWN), shard(1, OWN), rd.at[3 * NP], c=1 - c)
    for k, (dy, dc) in enumerate(yc_peers):
        start(wtb.at[me], wtb.at[me], rw.at[k], y=at(y + dy, NY), c=at(c + dc, NC))

    def got(s, p):
        part = piece(0, s, *parts[p])
        arrived(part, ra.at[slot(s, p)])
        if s == MINUS and p in (P1, P3):
            to_up(s, p)
        if s == PLUS and p in (P2, P4):
            to_down(s, p)
        if p in (P1, P2):
            sub = piece(0, s, k0, 256, 512) if p == P1 else part
            start(sub, sub, ra.at[slot(s, R1 if p == P1 else R2)], x=left)
            start(sub, sub, ra.at[slot(s, L1 if p == P1 else L2)], x=right)
            if p == P1:
                start(part, part, ra.at[slot(s, ZU)], z=below)
            else:
                start(part, part, ra.at[slot(s, ZD)], z=above)
        start(part, piece(1, s, *parts[p]), rd.at[slot(s, p)], c=1 - c)

    def from_partner(*ss):
        for s in ss:
            for p in range(NP):
                arrived(piece(1, s, *parts[p]), rd.at[slot(s, p)])

    def logits(lo, hi):
        prob[lo:hi, :] = lax.dot_general(
            hid[lo:hi, :], emb[...], (((1,), (1,)), ((), ())), preferred_element_type=f32
        )

    def over_rows(k, pair):
        return jnp.broadcast_to(jnp.concatenate(pair, 1), (128, 128)).T

    for s, p in ((PLUS, P2), (MINUS, P1), (PLUS, P4), (MINUS, P3), (MINUS, P2), (PLUS, P1), (MINUS, P4), (PLUS, P3)):
        got(s, p)

    for k, (dy, dc) in enumerate(yc_peers):
        arrived(wtb.at[at(c - dc, NC) * NY + at(y - dy, NY)], rw.at[k])
    for k in range(TOKENS // 128):
        ga, gb = group(*RHO[2 * k]), group(*RHO[2 * k + 1])
        wrep[128 * k : 128 * k + 128, :] = over_rows(k, [wtb[g, 0:1, 0:ROWS] for g in (ga, gb)])
        trep[128 * k : 128 * k + 128, :] = over_rows(k, [wtb[g, 1:2, 0:ROWS] for g in (ga, gb)])

    for s, p in (
        (PLUS, R2), (PLUS, L2), (PLUS, ZD), (MINUS, R1), (MINUS, L1), (MINUS, ZU),
        (FAR, P2), (FAR, P1), (FAR, P4), (FAR, P3),
        (MINUS, R2), (MINUS, L2), (MINUS, ZD), (PLUS, ZU), (PLUS, R1), (PLUS, L1),
    ):
        got(s, p)
    for load in load_emb:
        load.wait()

    base = ((((y * NC + c) * NX + x) * NZ + z) * VROWS).astype(f32)

    def exps(i, carry):
        r = pl.ds(pl.multiple_of(i * 32, 32), 32)
        t = jnp.tanh(prob[r, :] * (1.0 / soft_cap))
        e = jnp.exp(soft_cap * t - soft_cap)
        q = 1.0 - t * t
        v = e * q
        prob[r, :] = v
        pm[r, :] = v.astype(bf16)
        want = trep[r, :] - base
        lane = lax.broadcasted_iota(jnp.int32, (32, 128), 1).astype(f32)
        total = jnp.zeros((32, 128), f32)
        found = jnp.zeros((32, 128), f32)
        for k in range(VROWS // 128):
            s = slice(128 * k, 128 * k + 128)
            hit = want == lane + float(128 * k)
            hm[r, s] = jnp.where(hit, 1.0, 0.0).astype(bf16)
            total = total + e[:, s]
            found = found + jnp.where(hit, q[:, s], 0.0)
        sums[r, :] = total
        hits[r, :] = found
        return carry

    logits(0, 192)
    for p in (R2, L2, ZD, R1, L1, ZU):
        got(FAR, p)
    arrived(shard(1, OWN), rd.at[3 * NP])
    from_partner(PLUS, MINUS)
    logits(320, 512)
    lax.fori_loop(0, 6, exps, 0)
    from_partner(FAR)
    logits(192, 320)
    lax.fori_loop(6, TOKENS // 32, exps, 0)

    for k in range(TOKENS // 128):
        r = slice(128 * k, 128 * k + 128)
        total = jnp.sum(sums[r, :].T, axis=0, keepdims=True)
        found = jnp.sum(hits[r, :].T, axis=0, keepdims=True)
        for j in range(2):
            lanes = slice(ROWS * j, ROWS * j + ROWS)
            stat[pl.ds(group(*RHO[2 * k + j]), 1), :] = jnp.concatenate([total[:, lanes], found[:, lanes]], 1)

    for k, (dy, dc) in enumerate(yc_peers):
        start(stat, b1.at[k], rb.at[k], y=at(y + dy, NY), c=at(c + dc, NC))
    blocks = [at(x + d, NX) for d in ORDER]

    def for_partner(m, buf, rbuf, sem):
        for i in range(NX):
            v = jnp.dot(m[HALF:, :], emb[:, cols(blocks[i])], preferred_element_type=f32).astype(bf16)
            buf[i, 0:192] = v[64:256]
            buf[i, 192:256] = v[0:64]
            start(buf.at[i], rbuf.at[i], sem.at[i], c=1 - c)

    for_partner(pm, asend, arecv, rda)
    n1 = len(yc_peers)
    total = stat[...]
    for k in range(n1):
        arrived(b1.at[k], rb.at[k])
        total = total + b1[k]
    stat2[...] = total
    for d in range(1, NX):
        start(stat2, b2.at[d - 1], rb.at[n1 + d - 1], x=at(x + d, NX))
    for i in range(NX):
        own[i] = jnp.dot(pm[:HALF, :], emb[:, cols(blocks[i])], preferred_element_type=f32)
    for_partner(hm, tsend, trecv, rdt)
    for d in range(1, NX):
        arrived(b2.at[d - 1], rb.at[n1 + d - 1])
        total = total + b2[d - 1]
    stat3[...] = total
    n2 = n1 + NX - 1
    for d in (4, 3, 5, 2, 6, 1, 7):
        start(stat3, b3.at[d - 1], rb.at[n2 + d - 1], z=at(z + d, NZ))
    for i in range(NX):
        town[i] = jnp.dot(hm[:HALF, :], emb[:, cols(blocks[i])], preferred_element_type=f32).astype(bf16)
    for i in range(NX):
        arrived(arecv.at[i], rda.at[i])
        own[i] = own[i] + arecv[i].astype(f32)
    for i in range(NX):
        arrived(trecv.at[i], rdt.at[i])
        town[i] = town[i] + trecv[i]
    for d in range(1, NZ):
        arrived(b3.at[d - 1], rb.at[n2 + d - 1])
        total = total + b3[d - 1]
    every = total[:, 0:ROWS]
    rate[...] = jnp.concatenate(
        [(1.0 + 2.0 * z_weight * (soft_cap + jnp.log(every))) / every, total[:, ROWS:]], 1
    )
    for k in range(TOKENS // 128):
        r = slice(128 * k, 128 * k + 128)
        pair = [rate[pl.ds(group(*RHO[2 * k + j]), 1), :] for j in range(2)]
        frep[r, :] = over_rows(k, [v[:, 0:ROWS] for v in pair]) * wrep[r, :]
        grep[r, :] = over_rows(k, [v[:, ROWS:] for v in pair]) * wrep[r, :]

    for i, d in enumerate(ORDER):

        def combine(m, carry, i=i):
            r = pl.ds(pl.multiple_of(m * 32, 32), 32)
            f, g = frep[r, :], grep[r, :]
            for k in range(BLK // 128):
                s = slice(128 * k, 128 * k + 128)
                own[i, r, s] = f * own[i, r, s] - g * town[i, r, s].astype(f32)
            return carry

        lax.fori_loop(0, HALF // 32, combine, 0)
        fy[0, i] = own[i, 192:208, :].astype(bf16)
        fy[1, i] = own[i, 208:224, :].astype(bf16)
        start(fy.at[0, i], fyr.at[0, i], rfy.at[i], y=up)
        start(fy.at[1, i], fyr.at[1, i], rfy.at[NX + i], y=down)
        if d == 2:
            for s in range(NY):
                fx[0, s] = own[i, 64 * s + 32 : 64 * s + 48, :].astype(bf16)
                fx[1, s] = own[i, 64 * s + 48 : 64 * s + 64, :].astype(bf16)
            start(fx.at[0], fxr.at[0], rfx.at[0], x=right)
            start(fx.at[1], fxr.at[1], rfx.at[1], x=left)

    def scores(i, carry):
        r = pl.ds(pl.multiple_of(i * 32, 32), 32)
        f, g = frep[r, :], grep[r, :]
        for k in range(VROWS // 128):
            s = slice(128 * k, 128 * k + 128)
            sc[r, s] = f * prob[r, s] - g * hm[r, s].astype(f32)
        return carry

    lax.fori_loop(0, TOKENS // 32, scores, 0)

    for side, (b, dev) in enumerate(((1, right), (2, left))):
        arrived(fxr.at[side], rfx.at[side])
        for s in range(NY):
            lo = 64 * s + 32
            a1, a2 = own[b, lo : lo + 16, :], own[b, lo + 16 : lo + 32, :]
            more = fxr[side, s].astype(f32)
            nx[side, s, 0:16] = (a1 + more if side == 0 else a1).astype(bf16)
            nx[side, s, 16:32] = (a2 + more if side == 1 else a2).astype(bf16)
        start(nx.at[side], nxr.at[side], rnx.at[side], x=dev)
    for i in range(NX):
        for side, (lo, dev) in enumerate(((64, up), (128, down))):
            arrived(fyr.at[side, i], rfy.at[side * NX + i])
            a1, a2 = own[i, lo : lo + 16, :], own[i, lo + 16 : lo + 32, :]
            more = fyr[side, i].astype(f32)
            ny[side, i, 0:16] = (a1 + more if side == 0 else a1).astype(bf16)
            ny[side, i, 16:32] = (a2 + more if side == 1 else a2).astype(bf16)
            start(ny.at[side, i], nyr.at[side, i], rny.at[side * NX + i], y=dev)

    for k in range(VROWS // 128):
        s = slice(128 * k, 128 * k + 128)
        sct[s, :] = sc[:, s].T.astype(bf16)

    def table(i):
        tg_out[:, i * BLK : (i + 1) * BLK] = jnp.dot(
            sct[...], hid[:, i * BLK : (i + 1) * BLK], preferred_element_type=f32
        ).astype(bf16)

    table(0)
    table(1)

    for i, d in enumerate(ORDER):
        total = own[i, 0:32, :]
        for side in range(2):
            arrived(nyr.at[side, i], rny.at[side * NX + i])
            total = total + nyr[side, i].astype(f32)
        if d:
            ys[d - 1] = total.astype(bf16)
            start(ys.at[d - 1], sy.at[d - 1], rty.at[d - 1], x=blocks[i])
        else:
            keep0 = total
    for side in range(2):
        arrived(nxr.at[side], rnx.at[side])

    def x_sum(s):
        return own[NX - 1, 64 * s + 32 : 64 * s + 64, :] + nxr[0, s].astype(f32) + nxr[1, s].astype(f32)

    for s, dy in ((FAR, 2), (PLUS, 1), (MINUS, 3)):
        xs2[dy - 1] = x_sum(s).astype(bf16)
        start(xs2.at[dy - 1], sx.at[dy - 1], rtx.at[dy - 1], y=where[s])
    half = NZ // 2
    zf[0:half] = keep0.reshape(half, ZR, BLK)
    zf[half:NZ] = x_sum(OWN).reshape(half, ZR, BLK)
    table(2)
    keep0 = zf[0:half]
    for d in range(1, NX):
        arrived(sy.at[d - 1], rty.at[d - 1])
        keep0 = keep0 + sy[d - 1].astype(f32).reshape(half, ZR, BLK)
    keep1 = zf[half:NZ]
    for d in range(1, NY):
        arrived(sx.at[d - 1], rtx.at[d - 1])
        keep1 = keep1 + sx[d - 1].astype(f32).reshape(half, ZR, BLK)

    zf[0:half] = keep0
    zf[half:NZ] = keep1
    zs[...] = zf[...].astype(bf16)
    for d in (4, 3, 5, 2, 6, 1, 7):
        zz = at(z + d, NZ)
        start(zs.at[zz], rz.at[d - 1], rzs.at[d - 1], z=zz)
    table(3)
    total = zf[z]
    for d in (1, 7, 2, 6, 3, 5, 4):
        arrived(rz.at[d - 1], rzs.at[d - 1])
        total = total + rz[d - 1].astype(f32)
    gz[z] = total.astype(bf16)
    for d in (4, 3, 5, 2, 6, 1, 7):
        start(gz.at[z], gz.at[z], rzg.at[d - 1], z=at(z + d, NZ))

    def on_to_x(d, zz):
        for dx in (2, 1, 3):
            start(gz.at[zz], gx.at[dx - 1, zz], rxg.at[(dx - 1) * NZ + d], x=at(x + dx, NX))

    on_to_x(0, z)
    for d in (1, 7, 2, 6, 3, 5, 4):
        arrived(gz.at[at(z - d, NZ)], rzg.at[d - 1])
        on_to_x(d, at(z - d, NZ))
    hg_out[:, cols(x)] = gz[...].reshape(ROWS, BLK)
    for dx in range(1, NX):
        for d in range(NZ):
            arrived(gx.at[dx - 1, at(z - d, NZ)], rxg.at[(dx - 1) * NZ + d])
        hg_out[:, cols(at(x - dx, NX))] = gx[dx - 1].reshape(ROWS, BLK)

    for copy in sends:
        copy.wait_send()


def body(hidden, embedding, targets, loss_weight):
    vm = pltpu.VMEM
    dma = pltpu.SemaphoreType.DMA
    inputs = (hidden, embedding, loss_weight.reshape(1, ROWS), targets.reshape(1, ROWS))
    return pl.pallas_call(
        kernel,
        out_shape=(
            jax.ShapeDtypeStruct((ROWS, D), bf16),
            jax.ShapeDtypeStruct((VROWS, D), bf16),
        ),
        in_specs=[pl.BlockSpec(memory_space=pl.ANY)] * 4,
        out_specs=(pl.BlockSpec(memory_space=pltpu.VMEM), pl.BlockSpec(memory_space=pltpu.VMEM)),
        scratch_shapes=[
            vm((1, ROWS), bf16),
            vm((1, ROWS), jnp.int32),
            vm((TOKENS, D), bf16),
            vm((VROWS, D), bf16),
            vm((NC * NY, 2, 128), f32),
            vm((TOKENS, 128), f32),
            vm((TOKENS, 128), f32),
            vm((TOKENS, VROWS), f32),
            vm((TOKENS, 128), f32),
            vm((TOKENS, 128), f32),
            vm((NC * NY, 128), f32),
            vm((NC * NY, 128), f32),
            vm((NC * NY, 128), f32),
            vm((NC * NY, 128), f32),
            vm((TOKENS, 128), f32),
            vm((TOKENS, 128), f32),
            vm((NY * NC - 1, NC * NY, 128), f32),
            vm((NX - 1, NC * NY, 128), f32),
            vm((NZ - 1, NC * NY, 128), f32),
            vm((TOKENS, VROWS), bf16),
            vm((TOKENS, VROWS), bf16),
            vm((TOKENS, VROWS), f32),
            vm((VROWS, TOKENS), bf16),
            vm((NX, HALF, BLK), f32),
            vm((NX, HALF, BLK), bf16),
            vm((NX, HALF, BLK), bf16),
            vm((NX, HALF, BLK), bf16),
            vm((NX, HALF, BLK), bf16),
            vm((NX, HALF, BLK), bf16),
            vm((2, NX, SUB // 2, BLK), bf16),
            vm((2, NX, SUB // 2, BLK), bf16),
            vm((2, NX, SUB, BLK), bf16),
            vm((2, NX, SUB, BLK), bf16),
            vm((2, NY, SUB // 2, BLK), bf16),
            vm((2, NY, SUB // 2, BLK), bf16),
            vm((2, NY, SUB, BLK), bf16),
            vm((2, NY, SUB, BLK), bf16),
            vm((NX - 1, SUB, BLK), bf16),
            vm((NY - 1, SUB, BLK), bf16),
            vm((NX - 1, SUB, BLK), bf16),
            vm((NY - 1, SUB, BLK), bf16),
            vm((NZ, ZR, BLK), f32),
            vm((NZ, ZR, BLK), bf16),
            vm((NZ - 1, ZR, BLK), bf16),
            vm((NZ, ZR, BLK), bf16),
            vm((NX - 1, NZ, ZR, BLK), bf16),
            dma((NX + 3,)),
            dma((180,)),
            dma((30,)),
            dma((31,)),
            dma((NY * NC - 1,)),
            dma((NY * NC + NX + NZ - 3,)),
            dma((NX,)),
            dma((NX,)),
            dma((2 * NX,)),
            dma((2 * NX,)),
            dma((2,)),
            dma((2,)),
            dma((NX - 1,)),
            dma((NY - 1,)),
            dma((NZ - 1,)),
            dma((NZ - 1,)),
            dma(((NX - 1) * NZ,)),
        ],
        compiler_params=pltpu.CompilerParams(collective_id=0, has_side_effects=True, vmem_limit_bytes=44 * 1024 * 1024),
        name="head_backward",
    )(*(pltpu.with_memory_space_constraint(a, pltpu.HBM) for a in inputs))


def solution(mesh):
    finer = Mesh(mesh.devices.reshape(NY, NC, NX, NZ), ("y", "c", "x", "z"))
    dp = ("y", "c")
    both = ("y", "c", "x", "z")
    return jax.shard_map(
        body,
        mesh=finer,
        in_specs=(P(dp, None), P(both, None), P(dp), P(dp)),
        out_specs=(P(dp, None), P(both, None)),
        check_vma=False,
    )
```

time: 80.4 us -> 78.3 us (0.974)
  Pallas kernels: 76.5 us -> 74.3 us
    pallas_call x1, Pallas kernels: 76.5 us -> 74.3 us  [body(): pl.pallas_call(kernel, out_shape=(jax.ShapeDtypeStruct((ROWS, D), bf16),...]
where the time goes in v3:
time: 78.3 us; the launch traced here: 78.2 us
  Pallas kernels  74.3 us (95%)
  local copies, waits for them, and re-layouts  3.21 us (4%)
    pallas_call x1, Pallas kernels, body(): pl.pallas_call(kernel, out_shape=(jax.ShapeDtypeStruct((ROWS, D), bf16),...  74.3 us
    unnamed x2, local copies, waits for them, and re-layouts  3.21 us

profile of v3, /device:TPU:2, one launch (start us, length us, event | category | flops | bytes accessed | tf_op | source)
XLA Modules:
  0.0 78.2 jit_solution(7105899637214490335)
XLA Ops:
  0.6 74.3 %head_backward.1 = (bf16[64,3584]{1,0:T(8,128)(2,1)S(1)}, bf16[768,3584]{1,0:T(8,128)(2,1)S(1)}) custom-call(bf16[64,3584]{1,0:T(8,128)(2,1)} %hid_in.1, bf16[768,3584]{1,0:T(8,128)(2,1)} %emb_in.1, bf16[1,64]{1,0:T(2,128)(2,1)} %bitcast.2, s32[1,64]{1,0:T(1,128)} %bitcast.3), custom_call_target="tpu_custom_call" | custom-call | tf_op jit(solution)/shard_map/head_backward/pallas_call | solution.py:405
  75.0 0.8 copy.8
  75.8 2.4 %copy.9 = bf16[768,3584]{1,0:T(8,128)(2,1)} copy(bf16[768,3584]{1,0:T(8,128)(2,1)S(1)} %get-tuple-element.5) | data formatting | bytes 11010048

commit v4 on v3

v4 whole, which is shorter than its diff:
```python
import functools

import jax
import jax.numpy as jnp
from jax import lax
from jax.experimental import pallas as pl
from jax.experimental.pallas import tpu as pltpu
from jax.sharding import Mesh
from jax.sharding import PartitionSpec as P

MESH = pl.DeviceIdType.MESH
f32, bf16 = jnp.float32, jnp.bfloat16

NY, NC, NX, NZ = 4, 2, 4, 8
D, VROWS, ROWS = 3584, 768, 64
TOKENS = ROWS * NY * NC
HALF = ROWS * NY
BLK = D // NX
SUB = ROWS // 2
ZR = ROWS // NZ
ORDER = (2, 1, 3, 0)

soft_cap = 30.0
z_weight = 0.002


class Field:
    pass


BUFS = ("fy", "fyr", "ny", "nyr", "fx", "fxr", "nx", "nxr", "ys", "xs2", "sy", "sx", "zf", "zs", "rz")
SEMS = ("rd2", "rfy", "rny", "rfx", "rnx", "rty", "rtx", "rzs")


def kernel(
    hid_in, emb_in, w_in, t_in, hg_out, tg_out,
    w_own, t_own, hid, emb, wtb, wall, trep, prob, sums, fe, fq, stat, stat2, stat3, rate, frep, hrep, b1, b2, b3,
    pm, hm, sc, sct, own, town, asend, arecv, tsend, trecv, gz, gx,
    local_sem, send_sem, ra, rd, rw, rb, rzg, rxg, *fields,
):
    A, T = Field(), Field()
    n = len(BUFS) + len(SEMS)
    for field, refs in ((A, fields[:n]), (T, fields[n:])):
        for name, ref in zip(BUFS + SEMS, refs):
            setattr(field, name, ref)
    A.own, A.send, A.recv, A.m = own, asend, arecv, pm
    T.own, T.send, T.recv, T.m = town, tsend, trecv, hm
    y, c, x, z = (lax.axis_index(a) for a in ("y", "c", "x", "z"))
    rem = lax.rem

    def at(i, n):
        return rem(i + n, n)

    up, down, far = at(y + 1, NY), at(y - 1, NY), at(y + 2, NY)
    right, left = at(x + 1, NX), at(x - 1, NX)
    above, below = at(z + 1, NZ), at(z - 1, NZ)
    OWN, PLUS, MINUS, FAR = range(4)
    where = {OWN: y, PLUS: up, MINUS: down, FAR: far}
    RHO = ((0, OWN), (0, PLUS), (0, MINUS), (0, FAR), (1, FAR), (1, OWN), (1, PLUS), (1, MINUS))
    row_of = {key: ROWS * k for k, key in enumerate(RHO)}
    me = c * NY + y

    def group(e, s):
        return (1 - c if e else c) * NY + where[s]

    sends = []

    def start(src, dst, rsem, **dev):
        copy = pltpu.make_async_remote_copy(
            src_ref=src, dst_ref=dst, send_sem=send_sem.at[len(sends)], recv_sem=rsem, device_id=dev, device_id_type=MESH
        )
        copy.start()
        sends.append(copy)

    def arrived(dst, rsem):
        pltpu.make_async_remote_copy(
            src_ref=dst, dst_ref=dst, send_sem=send_sem.at[0], recv_sem=rsem, device_id={"c": 1 - c}, device_id_type=MESH
        ).wait_recv()

    def cols(q):
        return pl.ds(pl.multiple_of(q * BLK, 128), BLK)

    def shard(e, s):
        return hid.at[row_of[e, s] : row_of[e, s] + ROWS]

    def piece(e, s, q, lo, hi):
        return hid.at[row_of[e, s] : row_of[e, s] + ROWS, pl.ds(pl.multiple_of(q * BLK + lo, 128), hi - lo)]

    load_own = [
        pltpu.make_async_copy(hid_in, shard(0, OWN), local_sem.at[NX]),
        pltpu.make_async_copy(w_in, w_own, local_sem.at[NX + 1]),
        pltpu.make_async_copy(t_in, t_own, local_sem.at[NX + 2]),
    ]
    load_emb = []
    for k in range(NX):
        part = pl.ds(k * (VROWS // NX), VROWS // NX)
        load_emb.append(pltpu.make_async_copy(emb_in.at[part], emb.at[part], local_sem.at[k]))
    for load in load_own + load_emb:
        load.start()

    barrier = pltpu.get_barrier_semaphore()
    yc_peers = [(dy, dc) for dy in range(NY) for dc in range(NC) if (dy, dc) != (0, 0)]
    for dy, dc in yc_peers:
        pl.semaphore_signal(barrier, inc=1, device_id={"y": at(y + dy, NY), "c": at(c + dc, NC)}, device_id_type=MESH)
    for d in range(1, NX):
        pl.semaphore_signal(barrier, inc=1, device_id={"x": at(x + d, NX)}, device_id_type=MESH)
    for d in range(1, NZ):
        pl.semaphore_signal(barrier, inc=1, device_id={"z": at(z + d, NZ)}, device_id_type=MESH)

    for load in load_own:
        load.wait()
    none = jnp.zeros((1, ROWS), f32)
    wtb[me] = jnp.concatenate(
        [jnp.concatenate([v, none], 1) for v in (w_own[...].astype(f32), t_own[...].astype(f32))], 0
    )

    pl.semaphore_wait(barrier, len(yc_peers) + NX - 1 + NZ - 1)

    k0 = rem(x + 2 * z, NX)
    kp, km, k2 = rem(k0 + 1, NX), rem(k0 + 3, NX), rem(k0 + 2, NX)
    P1, P2, P3, P4, R1, R2, L1, L2, ZU, ZD = range(10)
    parts = (
        (k0, 0, 512), (k0, 512, BLK), (kp, 0, 256), (km, 0, 256),
        (kp, 256, 512), (kp, 512, BLK), (km, 256, 512), (km, 512, BLK),
        (k2, 0, 512), (k2, 512, BLK),
    )
    NP = len(parts)

    def slot(s, p):
        return (s - 1) * NP + p

    def to_up(s, p):
        start(piece(0, s, *parts[p]), piece(0, MINUS if s == OWN else FAR, *parts[p]), ra.at[slot(MINUS if s == OWN else FAR, p)], y=up)

    def to_down(s, p):
        start(piece(0, s, *parts[p]), piece(0, PLUS if s == OWN else FAR, *parts[p]), ra.at[slot(PLUS if s == OWN else FAR, p)], y=down)

    for k, (dy, dc) in enumerate(yc_peers):
        start(wtb.at[me], wtb.at[me], rw.at[k], y=at(y + dy, NY), c=at(c + dc, NC))
    for p, q in ((P1, P2), (P3, P4), (P2, P1), (P4, P3)):
        to_up(OWN, p)
        to_down(OWN, q)
    start(shard(0, OWN), shard(1, OWN), rd.at[3 * NP], c=1 - c)

    def got(s, p):
        part = piece(0, s, *parts[p])
        arrived(part, ra.at[slot(s, p)])
        if s == MINUS and p in (P1, P3):
            to_up(s, p)
        if s == PLUS and p in (P2, P4):
            to_down(s, p)
        if p in (P1, P2):
            sub = piece(0, s, k0, 256, 512) if p == P1 else part
            start(sub, sub, ra.at[slot(s, R1 if p == P1 else R2)], x=left)
            start(sub, sub, ra.at[slot(s, L1 if p == P1 else L2)], x=right)
            if p == P1:
                start(part, part, ra.at[slot(s, ZU)], z=below)
            else:
                start(part, part, ra.at[slot(s, ZD)], z=above)
        start(part, piece(1, s, *parts[p]), rd.at[slot(s, p)], c=1 - c)

    def from_partner(*ss):
        for s in ss:
            for p in range(NP):
                arrived(piece(1, s, *parts[p]), rd.at[slot(s, p)])

    def logits(lo, hi):
        prob[lo:hi, :] = lax.dot_general(
            hid[lo:hi, :], emb[...], (((1,), (1,)), ((), ())), preferred_element_type=f32
        )

    def over_rows(pair):
        return jnp.broadcast_to(jnp.concatenate(pair, 1), (128, 128)).T

    for s, p in ((PLUS, P2), (MINUS, P1)):
        got(s, p)

    for load in load_emb:
        load.wait()
    for k, (dy, dc) in enumerate(yc_peers):
        arrived(wtb.at[at(c - dc, NC) * NY + at(y - dy, NY)], rw.at[k])
    for k in range(TOKENS // 128):
        trep[128 * k : 128 * k + 128, :] = over_rows([wtb[group(*RHO[2 * k + j]), 1:2, 0:ROWS] for j in range(2)])
    for g in range(NC * NY):
        wall[g : g + 1, :] = wtb[g, 0:1, :]

    base = ((((y * NC + c) * NX + x) * NZ + z) * VROWS).astype(f32)

    def onehots(i, carry):
        r = pl.ds(pl.multiple_of(i * 32, 32), 32)
        want = trep[r, :] - base
        lane = lax.broadcasted_iota(jnp.int32, (32, 128), 1).astype(f32)
        for k in range(VROWS // 128):
            s = slice(128 * k, 128 * k + 128)
            hm[r, s] = jnp.where(want == lane + float(128 * k), 1.0, 0.0).astype(bf16)
        return carry

    lax.fori_loop(0, TOKENS // 32, onehots, 0)

    blocks = [at(x + d, NX) for d in ORDER]

    def for_partner(F, i):
        v = jnp.dot(F.m[HALF:, :], emb[:, cols(blocks[i])], preferred_element_type=f32).astype(bf16)
        F.send[i, 0:192] = v[64:256]
        F.send[i, 192:256] = v[0:64]
        start(F.send.at[i], F.recv.at[i], F.rd2.at[i], c=1 - c)

    def for_self(F, i):
        F.own[i] = jnp.dot(F.m[:HALF, :], emb[:, cols(blocks[i])], preferred_element_type=f32).astype(F.own.dtype)

    def of_chip(F, i):
        arrived(F.recv.at[i], F.rd2.at[i])
        F.own[i] = F.own[i] + F.recv[i].astype(F.own.dtype)

    def far_halves(F, i):
        F.fy[0, i] = F.own[i, 192:208, :].astype(bf16)
        F.fy[1, i] = F.own[i, 208:224, :].astype(bf16)
        start(F.fy.at[0, i], F.fyr.at[0, i], F.rfy.at[i], y=up)
        start(F.fy.at[1, i], F.fyr.at[1, i], F.rfy.at[NX + i], y=down)
        if ORDER[i] == 2:
            for s in range(NY):
                F.fx[0, s] = F.own[i, 64 * s + 32 : 64 * s + 48, :].astype(bf16)
                F.fx[1, s] = F.own[i, 64 * s + 48 : 64 * s + 64, :].astype(bf16)
            start(F.fx.at[0], F.fxr.at[0], F.rfx.at[0], x=right)
            start(F.fx.at[1], F.fxr.at[1], F.rfx.at[1], x=left)

    def with_far(F, i, lo, side, more):
        a1 = F.own[i, lo : lo + 16, :].astype(f32)
        a2 = F.own[i, lo + 16 : lo + 32, :].astype(f32)
        more = more.astype(f32)
        return (a1 + more if side == 0 else a1).astype(bf16), (a2 + more if side == 1 else a2).astype(bf16)

    def near_x(F):
        for side, (b, dev) in enumerate(((1, right), (2, left))):
            arrived(F.fxr.at[side], F.rfx.at[side])
            for s in range(NY):
                F.nx[side, s, 0:16], F.nx[side, s, 16:32] = with_far(F, b, 64 * s + 32, side, F.fxr[side, s])
            start(F.nx.at[side], F.nxr.at[side], F.rnx.at[side], x=dev)

    def near_y(F, i):
        for side, (lo, dev) in enumerate(((64, up), (128, down))):
            arrived(F.fyr.at[side, i], F.rfy.at[side * NX + i])
            F.ny[side, i, 0:16], F.ny[side, i, 16:32] = with_far(F, i, lo, side, F.fyr[side, i])
            start(F.ny.at[side, i], F.nyr.at[side, i], F.rny.at[side * NX + i], y=dev)

    half = NZ // 2

    def stage_two(F):
        for i, d in enumerate(ORDER):
            total = F.own[i, 0:32, :].astype(f32)
            for side in range(2):
                arrived(F.nyr.at[side, i], F.rny.at[side * NX + i])
                total = total + F.nyr[side, i].astype(f32)
            if d:
                F.ys[d - 1] = total.astype(bf16)
                start(F.ys.at[d - 1], F.sy.at[d - 1], F.rty.at[d - 1], x=blocks[i])
            else:
                F.zf[0:half] = total.reshape(half, ZR, BLK)
        for side in range(2):
            arrived(F.nxr.at[side], F.rnx.at[side])
        for s, dy in ((FAR, 2), (PLUS, 1), (MINUS, 3), (OWN, 0)):
            total = F.own[NX - 1, 64 * s_row[s] + 32 : 64 * s_row[s] + 64, :].astype(f32)
            total = total + F.nxr[0, s_row[s]].astype(f32) + F.nxr[1, s_row[s]].astype(f32)
            if dy:
                F.xs2[dy - 1] = total.astype(bf16)
                start(F.xs2.at[dy - 1], F.sx.at[dy - 1], F.rtx.at[dy - 1], y=where[s])
            else:
                F.zf[half:NZ] = total.reshape(half, ZR, BLK)

    s_row = {s: row_of[0, s] // ROWS for s in range(4)}

    def to_z(F):
        total = F.zf[0:half]
        for d in range(1, NX):
            arrived(F.sy.at[d - 1], F.rty.at[d - 1])
            total = total + F.sy[d - 1].astype(f32).reshape(half, ZR, BLK)
        F.zf[0:half] = total
        F.zs[0:half] = total.astype(bf16)
        total = F.zf[half:NZ]
        for d in range(1, NY):
            arrived(F.sx.at[d - 1], F.rtx.at[d - 1])
            total = total + F.sx[d - 1].astype(f32).reshape(half, ZR, BLK)
        F.zf[half:NZ] = total
        F.zs[half:NZ] = total.astype(bf16)
        for d in (4, 3, 5, 2, 6, 1, 7):
            zz = at(z + d, NZ)
            start(F.zs.at[zz], F.rz.at[d - 1], F.rzs.at[d - 1], z=zz)

    def z_sum(F):
        total = F.zf[z]
        for d in (1, 7, 2, 6, 3, 5, 4):
            arrived(F.rz.at[d - 1], F.rzs.at[d - 1])
            total = total + F.rz[d - 1].astype(f32)
        return total

    def exps(i, carry):
        r = pl.ds(pl.multiple_of(i * 32, 32), 32)
        t = jnp.tanh(prob[r, :] * (1.0 / soft_cap))
        e = jnp.exp(soft_cap * t - soft_cap)
        q = 1.0 - t * t
        total = jnp.zeros((32, 128), f32)
        found_e = jnp.zeros((32, 128), f32)
        found_q = jnp.zeros((32, 128), f32)
        for k in range(VROWS // 128):
            s = slice(128 * k, 128 * k + 128)
            hit = hm[r, s].astype(f32) > 0.5
            v = jnp.where(hit, 0.0, e[:, s] * q[:, s])
            prob[r, s] = v
            pm[r, s] = v.astype(bf16)
            total = total + e[:, s]
            found_e = found_e + jnp.where(hit, e[:, s], 0.0)
            found_q = found_q + jnp.where(hit, q[:, s], 0.0)
        sums[r, :] = total
        fe[r, :] = found_e
        fq[r, :] = found_q
        return carry

    for k, step in enumerate((
        ((PLUS, P4), (MINUS, P3)), ((MINUS, P2), (PLUS, P1)), ((MINUS, P4), (PLUS, P3)),
        ((PLUS, R2), (PLUS, L2), (PLUS, ZD)), ((MINUS, R1), (MINUS, L1), (MINUS, ZU), (FAR, P2)),
        ((FAR, P1), (FAR, P4)), ((FAR, P3), (MINUS, R2), (MINUS, L2), (MINUS, ZD)), ((PLUS, ZU), (PLUS, R1), (PLUS, L1)),
    )):
        for s, p in step:
            got(s, p)
        if k < NX:
            for_partner(T, k)
        else:
            for_self(T, k - NX)
            of_chip(T, k - NX)
            far_halves(T, k - NX)
    logits(0, 192)
    for p in (R2, L2, ZD, R1, L1, ZU):
        got(FAR, p)
    arrived(shard(1, OWN), rd.at[3 * NP])
    from_partner(PLUS, MINUS)
    logits(320, 512)
    near_x(T)
    for i in range(NX):
        near_y(T, i)
    from_partner(FAR)
    logits(192, 320)
    lax.fori_loop(0, TOKENS // 32, exps, 0)

    def stats():
        for k in range(TOKENS // 128):
            r = slice(128 * k, 128 * k + 128)
            three = [jnp.sum(v[r, :].T, axis=0, keepdims=True) for v in (sums, fe, fq)]
            for j in range(2):
                lanes = slice(ROWS * j, ROWS * j + ROWS)
                stat[pl.ds(group(*RHO[2 * k + j]), 1), :] = jnp.concatenate([v[:, lanes] for v in three] + [none], 1)
        for k, (dy, dc) in enumerate(yc_peers):
            start(stat, b1.at[k], rb.at[k], y=at(y + dy, NY), c=at(c + dc, NC))

    n1 = len(yc_peers)
    n2 = n1 + NX - 1
    for_partner(A, 0)
    stats()
    for_partner(A, 1)
    for_self(A, 0)
    of_chip(A, 0)
    far_halves(A, 0)
    for_partner(A, 2)
    for_self(A, 1)
    of_chip(A, 1)
    far_halves(A, 1)
    total = stat[...]
    for k in range(n1):
        arrived(b1.at[k], rb.at[k])
        total = total + b1[k]
    stat2[...] = total
    for d in range(1, NX):
        start(stat2, b2.at[d - 1], rb.at[n1 + d - 1], x=at(x + d, NX))
    for_partner(A, 3)
    for_self(A, 2)
    of_chip(A, 2)
    far_halves(A, 2)
    stage_two(T)
    for_self(A, 3)
    of_chip(A, 3)
    far_halves(A, 3)
    total = stat2[...]
    for d in range(1, NX):
        arrived(b2.at[d - 1], rb.at[n1 + d - 1])
        total = total + b2[d - 1]
    stat3[...] = total
    for d in (4, 3, 5, 2, 6, 1, 7):
        start(stat3, b3.at[d - 1], rb.at[n2 + d - 1], z=at(z + d, NZ))
    near_x(A)
    for i in range(NX):
        near_y(A, i)
    to_z(T)

    total = stat3[...]
    for d in range(1, NZ):
        arrived(b3.at[d - 1], rb.at[n2 + d - 1])
        total = total + b3[d - 1]
    every, e_hit, q_hit = (total[:, ROWS * k : ROWS * k + ROWS] for k in range(3))
    w = wall[:, 0:ROWS]
    factor = w * (1.0 + 2.0 * z_weight * (soft_cap + jnp.log(every))) / every
    rate[...] = jnp.concatenate([factor, (factor * e_hit - w) * q_hit], 1)
    for k in range(TOKENS // 128):
        r = slice(128 * k, 128 * k + 128)
        pair = [rate[pl.ds(group(*RHO[2 * k + j]), 1), :] for j in range(2)]
        frep[r, :] = over_rows([v[:, 0:ROWS] for v in pair])
        hrep[r, :] = over_rows([v[:, ROWS:] for v in pair])

    def scores(i, carry):
        r = pl.ds(pl.multiple_of(i * 32, 32), 32)
        f, h = frep[r, :], hrep[r, :]
        for k in range(VROWS // 128):
            s = slice(128 * k, 128 * k + 128)
            sc[r, s] = f * prob[r, s] + h * hm[r, s].astype(f32)
        return carry

    def table(i):
        tg_out[:, i * BLK : (i + 1) * BLK] = jnp.dot(
            sct[...], hid[:, i * BLK : (i + 1) * BLK], preferred_element_type=f32
        ).astype(bf16)

    lax.fori_loop(0, TOKENS // 32, scores, 0)
    for k in range(VROWS // 128):
        s = slice(128 * k, 128 * k + 128)
        sct[s, :] = sc[:, s].T.astype(bf16)
    table(0)
    table(1)
    stage_two(A)
    table(2)
    table(3)
    to_z(A)
    mine = pl.ds(pl.multiple_of(z * ZR, ZR), ZR)
    t_part = z_sum(T)
    a_part = z_sum(A)
    f, h = frep[mine, :], hrep[mine, :]
    for k in range(BLK // 128):
        s = slice(128 * k, 128 * k + 128)
        gz[z, :, s] = (f * a_part[:, s] + h * t_part[:, s]).astype(bf16)
    for d in (4, 3, 5, 2, 6, 1, 7):
        start(gz.at[z], gz.at[z], rzg.at[d - 1], z=at(z + d, NZ))

    def on_to_x(d, zz):
        for dx in (2, 1, 3):
            start(gz.at[zz], gx.at[dx - 1, zz], rxg.at[(dx - 1) * NZ + d], x=at(x + dx, NX))

    on_to_x(0, z)
    for d in (1, 7, 2, 6, 3, 5, 4):
        arrived(gz.at[at(z - d, NZ)], rzg.at[d - 1])
        on_to_x(d, at(z - d, NZ))
    hg_out[:, cols(x)] = gz[...].reshape(ROWS, BLK)
    for dx in range(1, NX):
        for d in range(NZ):
            arrived(gx.at[dx - 1, at(z - d, NZ)], rxg.at[(dx - 1) * NZ + d])
        hg_out[:, cols(at(x - dx, NX))] = gx[dx - 1].reshape(ROWS, BLK)

    for copy in sends:
        copy.wait_send()


def body(hidden, embedding, targets, loss_weight):
    vm = pltpu.VMEM
    dma = pltpu.SemaphoreType.DMA
    inputs = (hidden, embedding, loss_weight.reshape(1, ROWS), targets.reshape(1, ROWS))
    return pl.pallas_call(
        kernel,
        out_shape=(
            jax.ShapeDtypeStruct((ROWS, D), bf16),
            jax.ShapeDtypeStruct((VROWS, D), bf16),
        ),
        in_specs=[pl.BlockSpec(memory_space=pl.ANY)] * 4,
        out_specs=(pl.BlockSpec(memory_space=pltpu.VMEM), pl.BlockSpec(memory_space=pltpu.VMEM)),
        scratch_shapes=[
            vm((1, ROWS), bf16),
            vm((1, ROWS), jnp.int32),
            vm((TOKENS, D), bf16),
            vm((VROWS, D), bf16),
            vm((NC * NY, 2, 128), f32),
            vm((NC * NY, 128), f32),
            vm((TOKENS, 128), f32),
            vm((TOKENS, VROWS), f32),
            vm((TOKENS, 128), f32),
            vm((TOKENS, 128), f32),
            vm((TOKENS, 128), f32),
            vm((NC * NY, 256), f32),
            vm((NC * NY, 256), f32),
            vm((NC * NY, 256), f32),
            vm((NC * NY, 128), f32),
            vm((TOKENS, 128), f32),
            vm((TOKENS, 128), f32),
            vm((NY * NC - 1, NC * NY, 256), f32),
            vm((NX - 1, NC * NY, 256), f32),
            vm((NZ - 1, NC * NY, 256), f32),
            vm((TOKENS, VROWS), bf16),
            vm((TOKENS, VROWS), bf16),
            vm((TOKENS, VROWS), f32),
            vm((VROWS, TOKENS), bf16),
            vm((NX, HALF, BLK), f32),
            vm((NX, HALF, BLK), bf16),
            vm((NX, HALF, BLK), bf16),
            vm((NX, HALF, BLK), bf16),
            vm((NX, HALF, BLK), bf16),
            vm((NX, HALF, BLK), bf16),
            vm((NZ, ZR, BLK), bf16),
            vm((NX - 1, NZ, ZR, BLK), bf16),
            dma((NX + 3,)),
            dma((230,)),
            dma((30,)),
            dma((31,)),
            dma((NY * NC - 1,)),
            dma((NY * NC + NX + NZ - 3,)),
            dma((NZ - 1,)),
            dma(((NX - 1) * NZ,)),
        ]
        + 2
        * [
            vm((2, NX, SUB // 2, BLK), bf16),
            vm((2, NX, SUB // 2, BLK), bf16),
            vm((2, NX, SUB, BLK), bf16),
            vm((2, NX, SUB, BLK), bf16),
            vm((2, NY, SUB // 2, BLK), bf16),
            vm((2, NY, SUB // 2, BLK), bf16),
            vm((2, NY, SUB, BLK), bf16),
            vm((2, NY, SUB, BLK), bf16),
            vm((NX - 1, SUB, BLK), bf16),
            vm((NY - 1, SUB, BLK), bf16),
            vm((NX - 1, SUB, BLK), bf16),
            vm((NY - 1, SUB, BLK), bf16),
            vm((NZ, ZR, BLK), f32),
            vm((NZ, ZR, BLK), bf16),
            vm((NZ - 1, ZR, BLK), bf16),
            dma((NX,)),
            dma((2 * NX,)),
            dma((2 * NX,)),
            dma((2,)),
            dma((2,)),
            dma((NX - 1,)),
            dma((NY - 1,)),
            dma((NZ - 1,)),
        ],
        compiler_params=pltpu.CompilerParams(collective_id=0, has_side_effects=True, vmem_limit_bytes=44 * 1024 * 1024),
        name="head_backward",
    )(*(pltpu.with_memory_space_constraint(a, pltpu.HBM) for a in inputs))


def solution(mesh):
    finer = Mesh(mesh.devices.reshape(NY, NC, NX, NZ), ("y", "c", "x", "z"))
    dp = ("y", "c")
    both = ("y", "c", "x", "z")
    return jax.shard_map(
        body,
        mesh=finer,
        in_specs=(P(dp, None), P(both, None), P(dp), P(dp)),
        out_specs=(P(dp, None), P(both, None)),
        check_vma=False,
    )
```

time: 78.3 us -> 72.9 us (0.931)
  Pallas kernels: 74.3 us -> 69 us
    pallas_call x1, Pallas kernels: 74.3 us -> 69 us  [body(): pl.pallas_call(kernel, out_shape=(jax.ShapeDtypeStruct((ROWS, D), bf16),...]
where the time goes in v4:
time: 72.9 us; the launch traced here: 72.8 us
  Pallas kernels  69 us (95%)
  local copies, waits for them, and re-layouts  3.21 us (4%)
    pallas_call x1, Pallas kernels, body(): pl.pallas_call(kernel, out_shape=(jax.ShapeDtypeStruct((ROWS, D), bf16),...  69 us
    unnamed x2, local copies, waits for them, and re-layouts  3.21 us

profile of v4, /device:TPU:2, one launch (start us, length us, event | category | flops | bytes accessed | tf_op | source)
XLA Modules:
  0.0 72.8 jit_solution(4318652844191276246)
XLA Ops:
  0.6 69.0 %head_backward.1 = (bf16[64,3584]{1,0:T(8,128)(2,1)S(1)}, bf16[768,3584]{1,0:T(8,128)(2,1)S(1)}) custom-call(bf16[64,3584]{1,0:T(8,128)(2,1)} %hid_in.1, bf16[768,3584]{1,0:T(8,128)(2,1)} %emb_in.1, bf16[1,64]{1,0:T(2,128)(2,1)} %bitcast.2, s32[1,64]{1,0:T(1,128)} %bitcast.3), custom_call_target="tpu_custom_call" | custom-call | tf_op jit(solution)/shard_map/head_backward/pallas_call | solution.py:462
  69.6 0.8 %copy.8 = bf16[64,3584]{1,0:T(8,128)(2,1)} copy(bf16[64,3584]{1,0:T(8,128)(2,1)S(1)} %get-tuple-element.4) | data formatting | bytes 917504
  70.4 2.4 %copy.9 = bf16[768,3584]{1,0:T(8,128)(2,1)} copy(bf16[768,3584]{1,0:T(8,128)(2,1)S(1)} %get-tuple-element.5) | data formatting | bytes 11010048

commit v5 on v4

--- a/solution.py
+++ b/solution.py
@@ -71,6 +71,13 @@
         )
         copy.start()
         sends.append(copy)
+
+    drained = []
+
+    def drain(until):
+        for copy in sends[len(drained) : until]:
+            copy.wait_send()
+            drained.append(copy)
 
     def arrived(dst, rsem):
         pltpu.make_async_remote_copy(
@@ -159,15 +166,16 @@
                 start(part, part, ra.at[slot(s, ZD)], z=above)
         start(part, piece(1, s, *parts[p]), rd.at[slot(s, p)], c=1 - c)
 
-    def from_partner(*ss):
-        for s in ss:
-            for p in range(NP):
+    def from_partner(*ps):
+        for p in ps:
+            for s in (PLUS, MINUS, FAR):
                 arrived(piece(1, s, *parts[p]), rd.at[slot(s, p)])
 
-    def logits(lo, hi):
-        prob[lo:hi, :] = lax.dot_general(
-            hid[lo:hi, :], emb[...], (((1,), (1,)), ((), ())), preferred_element_type=f32
+    def logits(q, first_one):
+        out = lax.dot_general(
+            hid[:, cols(q)], emb[:, cols(q)], (((1,), (1,)), ((), ())), preferred_element_type=f32
         )
+        prob[...] = out if first_one else prob[...] + out
 
     def over_rows(pair):
         return jnp.broadcast_to(jnp.concatenate(pair, 1), (128, 128)).T
@@ -199,14 +207,12 @@
 
     blocks = [at(x + d, NX) for d in ORDER]
 
-    def for_partner(F, i):
-        v = jnp.dot(F.m[HALF:, :], emb[:, cols(blocks[i])], preferred_element_type=f32).astype(bf16)
-        F.send[i, 0:192] = v[64:256]
-        F.send[i, 192:256] = v[0:64]
+    def product(F, i):
+        v = jnp.dot(F.m[...], emb[:, cols(blocks[i])], preferred_element_type=f32)
+        F.send[i, 0:192] = v[HALF + 64 :].astype(bf16)
+        F.send[i, 192:256] = v[HALF : HALF + 64].astype(bf16)
         start(F.send.at[i], F.recv.at[i], F.rd2.at[i], c=1 - c)
-
-    def for_self(F, i):
-        F.own[i] = jnp.dot(F.m[:HALF, :], emb[:, cols(blocks[i])], preferred_element_type=f32).astype(F.own.dtype)
+        F.own[i] = v[:HALF].astype(F.own.dtype)
 
     def of_chip(F, i):
         arrived(F.recv.at[i], F.rd2.at[i])
@@ -316,30 +322,34 @@
         return carry
 
     for k, step in enumerate((
-        ((PLUS, P4), (MINUS, P3)), ((MINUS, P2), (PLUS, P1)), ((MINUS, P4), (PLUS, P3)),
-        ((PLUS, R2), (PLUS, L2), (PLUS, ZD)), ((MINUS, R1), (MINUS, L1), (MINUS, ZU), (FAR, P2)),
-        ((FAR, P1), (FAR, P4)), ((FAR, P3), (MINUS, R2), (MINUS, L2), (MINUS, ZD)), ((PLUS, ZU), (PLUS, R1), (PLUS, L1)),
+        ((PLUS, P4), (MINUS, P3), (MINUS, P2), (PLUS, P1)), ((MINUS, P4), (PLUS, P3), (PLUS, R2), (PLUS, L2), (PLUS, ZD)),
+        ((MINUS, R1), (MINUS, L1), (MINUS, ZU), (FAR, P2), (FAR, P1)), ((FAR, P4), (FAR, P3)),
     )):
         for s, p in step:
             got(s, p)
-        if k < NX:
-            for_partner(T, k)
-        else:
-            for_self(T, k - NX)
-            of_chip(T, k - NX)
-            far_halves(T, k - NX)
-    logits(0, 192)
+        product(T, k)
+    for s, p in ((MINUS, R2), (MINUS, L2), (MINUS, ZD), (PLUS, ZU), (PLUS, R1), (PLUS, L1)):
+        got(s, p)
+    arrived(shard(1, OWN), rd.at[3 * NP])
+    from_partner(P1, P2)
+    logits(k0, True)
+    for i in range(NX):
+        of_chip(T, i)
+        far_halves(T, i)
     for p in (R2, L2, ZD, R1, L1, ZU):
         got(FAR, p)
-    arrived(shard(1, OWN), rd.at[3 * NP])
-    from_partner(PLUS, MINUS)
-    logits(320, 512)
+    from_partner(P3, R2, R1)
+    logits(kp, False)
+    from_partner(P4, L2, L1)
+    logits(km, False)
     near_x(T)
     for i in range(NX):
         near_y(T, i)
-    from_partner(FAR)
-    logits(192, 320)
+    from_partner(ZD, ZU)
+    logits(k2, False)
     lax.fori_loop(0, TOKENS // 32, exps, 0)
+
+    first_part = len(sends)
 
     def stats():
         for k in range(TOKENS // 128):
@@ -353,16 +363,18 @@
 
     n1 = len(yc_peers)
     n2 = n1 + NX - 1
-    for_partner(A, 0)
+    product(A, 0)
     stats()
-    for_partner(A, 1)
-    for_self(A, 0)
+    product(A, 1)
+    product(A, 2)
     of_chip(A, 0)
     far_halves(A, 0)
-    for_partner(A, 2)
-    for_self(A, 1)
-    of_chip(A, 1)
-    far_halves(A, 1)
+    product(A, 3)
+    for i in (1, 2):
+        of_chip(A, i)
+        far_halves(A, i)
+    of_chip(A, 3)
+    far_halves(A, 3)
     total = stat[...]
     for k in range(n1):
         arrived(b1.at[k], rb.at[k])
@@ -370,14 +382,10 @@
     stat2[...] = total
     for d in range(1, NX):
         start(stat2, b2.at[d - 1], rb.at[n1 + d - 1], x=at(x + d, NX))
-    for_partner(A, 3)
-    for_self(A, 2)
-    of_chip(A, 2)
-    far_halves(A, 2)
-    stage_two(T)
-    for_self(A, 3)
-    of_chip(A, 3)
-    far_halves(A, 3)
+    near_x(A)
+    near_y(A, 0)
+    for i in range(1, NX):
+        near_y(A, i)
     total = stat2[...]
     for d in range(1, NX):
         arrived(b2.at[d - 1], rb.at[n1 + d - 1])
@@ -385,10 +393,9 @@
     stat3[...] = total
     for d in (4, 3, 5, 2, 6, 1, 7):
         start(stat3, b3.at[d - 1], rb.at[n2 + d - 1], z=at(z + d, NZ))
-    near_x(A)
-    for i in range(NX):
-        near_y(A, i)
-    to_z(T)
+    second_part = len(sends)
+    stage_two(T)
+    drain(first_part)
 
     total = stat3[...]
     for d in range(1, NZ):
@@ -422,11 +429,13 @@
         s = slice(128 * k, 128 * k + 128)
         sct[s, :] = sc[:, s].T.astype(bf16)
     table(0)
+    stage_two(A)
+    to_z(T)
     table(1)
-    stage_two(A)
     table(2)
+    to_z(A)
     table(3)
-    to_z(A)
+    drain(second_part)
     mine = pl.ds(pl.multiple_of(z * ZR, ZR), ZR)
     t_part = z_sum(T)
     a_part = z_sum(A)
@@ -451,8 +460,7 @@
             arrived(gx.at[dx - 1, at(z - d, NZ)], rxg.at[(dx - 1) * NZ + d])
         hg_out[:, cols(at(x - dx, NX))] = gx[dx - 1].reshape(ROWS, BLK)
 
-    for copy in sends:
-        copy.wait_send()
+    drain(len(sends))
 
 
 def body(hidden, embedding, targets, loss_weight):

time: 72.9 us -> 71.3 us (0.978)
  Pallas kernels: 69 us -> 67.3 us
    pallas_call x1, Pallas kernels: 69 us -> 67.3 us  [body(): pl.pallas_call(kernel, out_shape=(jax.ShapeDtypeStruct((ROWS, D), bf16),...]
where the time goes in v5:
time: 71.3 us; the launch traced here: 71.2 us
  Pallas kernels  67.3 us (94%)
  local copies, waits for them, and re-layouts  3.21 us (5%)
    pallas_call x1, Pallas kernels, body(): pl.pallas_call(kernel, out_shape=(jax.ShapeDtypeStruct((ROWS, D), bf16),...  67.3 us
    unnamed x2, local copies, waits for them, and re-layouts  3.21 us

profile of v5, /device:TPU:2, one launch (start us, length us, event | category | flops | bytes accessed | tf_op | source)
XLA Modules:
  0.0 71.2 jit_solution(2647238529826345210)
XLA Ops:
  0.6 67.3 %head_backward.1 = (bf16[64,3584]{1,0:T(8,128)(2,1)S(1)}, bf16[768,3584]{1,0:T(8,128)(2,1)S(1)}) custom-call(bf16[64,3584]{1,0:T(8,128)(2,1)} %hid_in.1, bf16[768,3584]{1,0:T(8,128)(2,1)} %emb_in.1, bf16[1,64]{1,0:T(2,128)(2,1)} %bitcast.2, s32[1,64]{1,0:T(1,128)} %bitcast.3), custom_call_target="tpu_custom_call" | custom-call | tf_op jit(solution)/shard_map/head_backward/pallas_call | solution.py:470
  68.0 0.8 %copy.8 = bf16[64,3584]{1,0:T(8,128)(2,1)} copy(bf16[64,3584]{1,0:T(8,128)(2,1)S(1)} %get-tuple-element.4) | data formatting | bytes 917504
  68.7 2.4 %copy.9 = bf16[768,3584]{1,0:T(8,128)(2,1)} copy(bf16[768,3584]{1,0:T(8,128)(2,1)S(1)} %get-tuple-element.5) | data formatting | bytes 11010048

commit v6 on v5

--- a/solution.py
+++ b/solution.py
@@ -443,7 +443,7 @@
     for k in range(BLK // 128):
         s = slice(128 * k, 128 * k + 128)
         gz[z, :, s] = (f * a_part[:, s] + h * t_part[:, s]).astype(bf16)
-    for d in (4, 3, 5, 2, 6, 1, 7):
+    for d in (1, 7, 2, 6, 3, 5, 4):
         start(gz.at[z], gz.at[z], rzg.at[d - 1], z=at(z + d, NZ))
 
     def on_to_x(d, zz):

time: 71.3 us -> 71 us (level)
  no operation moved by 1% of the time
where the time goes in v6:
time: 71 us; the launch traced here: 70.9 us
  Pallas kernels  67.1 us (95%)
  local copies, waits for them, and re-layouts  3.21 us (5%)
    pallas_call x1, Pallas kernels, body(): pl.pallas_call(kernel, out_shape=(jax.ShapeDtypeStruct((ROWS, D), bf16),...  67.1 us
    unnamed x2, local copies, waits for them, and re-layouts  3.21 us

profile of v6, /device:TPU:2, one launch (start us, length us, event | category | flops | bytes accessed | tf_op | source)
XLA Modules:
  0.0 70.9 jit_solution(6510625644919703175)
XLA Ops:
  0.6 67.1 %head_backward.1 = (bf16[64,3584]{1,0:T(8,128)(2,1)S(1)}, bf16[768,3584]{1,0:T(8,128)(2,1)S(1)}) custom-call(bf16[64,3584]{1,0:T(8,128)(2,1)} %hid_in.1, bf16[768,3584]{1,0:T(8,128)(2,1)} %emb_in.1, bf16[1,64]{1,0:T(2,128)(2,1)} %bitcast.2, s32[1,64]{1,0:T(1,128)} %bitcast.3), custom_call_target="tpu_custom_call" | custom-call | tf_op jit(solution)/shard_map/head_backward/pallas_call | solution.py:470
  67.7 0.8 %copy.8 = bf16[64,3584]{1,0:T(8,128)(2,1)} copy(bf16[64,3584]{1,0:T(8,128)(2,1)S(1)} %get-tuple-element.4) | data formatting | bytes 917504
  68.5 2.4 %copy.9 = bf16[768,3584]{1,0:T(8,128)(2,1)} copy(bf16[768,3584]{1,0:T(8,128)(2,1)S(1)} %get-tuple-element.5) | data formatting | bytes 11010048
